TPU v7x, 8 devices: a whole 2x2x1 slice. The times are simulated.
8 devices in a mesh: dp: 1 (over z), sp: 8 (over y, x, core).
Axes of the slice: x: 2, y: 2, z: 1, core: 2. Of those that a mesh axis runs over, the one named last changes fastest.
Arguments:
- patches: bfloat16 [8192, 1280], P(('dp', 'sp'))
- embeds: bfloat16 [4096, 1536], P(('dp', 'sp'))
- dest_slot: int32 [2048], P(('dp', 'sp'))
- rope_pos: int32 [3, 4096], P(None, ('dp', 'sp'))
- cu_doc: int32 [3], P('dp')
- ln_w: bfloat16 [1280], replicated
- ln_b: bfloat16 [1280], replicated
- w_one: bfloat16 [5120, 5120], replicated
- b_one: bfloat16 [5120], replicated
- w_two: bfloat16 [5120, 1536], replicated
- b_two: bfloat16 [1536], replicated
- norm_attn: bfloat16 [1536], replicated
- w_q: bfloat16 [1536, 1536], replicated
- b_q: bfloat16 [1536], replicated
- w_k: bfloat16 [1536, 256], replicated
- b_k: bfloat16 [256], replicated
- w_v: bfloat16 [1536, 256], replicated
- b_v: bfloat16 [256], replicated
- w_o: bfloat16 [1536, 1536], replicated
- norm_mlp: bfloat16 [1536], replicated
- w_gate: bfloat16 [1536, 8960], replicated
- w_up: bfloat16 [1536, 8960], replicated
- w_down: bfloat16 [8960, 1536], replicated
Outputs:
- output: bfloat16 [4096, 1536], P(('dp', 'sp'))
All inputs are finite; a program needn't handle non-finite values.
Results may differ from a plain program's by a relative error of at most 0.0107451.
Values are sent between devices in bfloat16 or wider.
A program may use at most 1 GiB of HBM per device.

v0:
```python
import functools
import jax
import jax.numpy as jnp
from jax import lax
from jax.experimental import pallas as pl
from jax.experimental.pallas import tpu as pltpu
from jax.sharding import PartitionSpec as P

BF = jnp.bfloat16
F32 = jnp.float32
MESH=pl.DeviceIdType.MESH
D=128
SC=D**-0.5*1.4426950408889634
def attn_body(n, nh, nkv, cu_ref, q_ref, kt_ref, v_ref, o_ref, qa, kb, vb, acc, mx, ls, ssem, rsem, fsem):
    T=q_ref.shape[0]; grp=nh//nkv
    ncut=cu_ref.shape[0]-2
    me=lax.axis_index('sp'); chip=me//2; core=lax.rem(me,2); partner=chip*2+1-core
    dev=lambda i: {'sp':i}
    bar=pltpu.get_barrier_semaphore()
    for d in range(1,n):
        pl.semaphore_signal(bar,inc=1,device_id=dev(lax.rem(me+d,n)),device_id_type=MESH)
    lane=lax.broadcasted_iota(jnp.int32,(T,D),1); rowq=lax.broadcasted_iota(jnp.int32,(T,D),0)+me*T
    tail=jnp.zeros((T,D),F32)
    for d in range(ncut):
        tail=jnp.where((lane==d)&(rowq>=cu_ref[1+d]),-1e30,tail)
    tail=tail.astype(BF)
    pl.semaphore_wait(bar,n-1)
    def rcopy(what,src_s,g,tgt,sem_s,sem_r,loc=False):
        if what==0:
            src=kt_ref.at[pl.ds(g*D,D),:] if loc else kb.at[src_s,g,pl.ds(0,D),:]
            dst=kb.at[src_s,g,pl.ds(0,D),:]
        else:
            src=v_ref.at[:,pl.ds(g*D,D)] if loc else vb.at[src_s,g]
            dst=vb.at[src_s,g]
        return pltpu.make_async_remote_copy(src_ref=src,dst_ref=dst,send_sem=sem_s,recv_sem=sem_r,device_id=dev(tgt),device_id_type=MESH)
    def my_send(dc,g,w):
        tgt=partner if dc==0 else me+2*dc
        return rcopy(w,me,g,tgt,ssem.at[dc,g,w],rsem.at[me,g,w],loc=True)
    def send_cond(dc):
        return (core==0) if dc==0 else (me+2*dc<n)
    for dc in range(n//2):
        @pl.when(send_cond(dc))
        def _(dc=dc):
            for g in range(nkv):
                for w in range(2): my_send(dc,g,w).start()
    def fill(s,_):
        krow=lax.broadcasted_iota(jnp.int32,(D,T),0); kpos=lax.broadcasted_iota(jnp.int32,(D,T),1)+s*T
        kt=jnp.zeros((D,T),F32)
        for d in range(ncut):
            kt=jnp.where((krow==d)&(kpos<cu_ref[1+d]),1.0,kt)
        kt=kt.astype(BF)
        for g in range(nkv): kb[s,g,pl.ds(D,D),:]=kt
        return 0
    lax.fori_loop(0,n,fill,0)
    for h in range(nh):
        qa[h,:,:D]=q_ref[:,h*D:(h+1)*D]
        qa[h,:,D:]=tail
    for g in range(nkv):
        kb[me,g,pl.ds(0,D),:]=kt_ref[g*D:(g+1)*D,:]
    HB=T//2
    def own(h,_):
        g=h//grp
        for r in range(2):
            rows=pl.ds(r*HB,HB); W=(r+1)*HB
            s=jnp.dot(qa[h,rows,:],kb[me,g,:,pl.ds(0,W)],preferred_element_type=F32)*SC
            qi=lax.broadcasted_iota(jnp.int32,(HB,W),0)+r*HB; ki=lax.broadcasted_iota(jnp.int32,(HB,W),1)
            s=jnp.where(ki<=qi,s,-1e30)
            m=jnp.max(s,axis=1,keepdims=True)
            p=jnp.exp2(s-m)
            l=p[:,:D]
            for j in range(1,W//D): l=l+p[:,j*D:(j+1)*D]
            mx[h,rows,:]=jnp.broadcast_to(m,(HB,D)); ls[h,rows,:]=l
            vg=v_ref[pl.ds(0,W),pl.ds(pl.multiple_of(g*D,D),D)]
            acc[h,rows,:]=jnp.dot(p.astype(BF),vg,preferred_element_type=F32)
        return 0
    lax.fori_loop(0,nh,own,0)
    def head_step(h,s,g):
        sc=jnp.dot(qa[h],kb[s,g],preferred_element_type=F32)*SC
        mp=mx[h]
        m=jnp.maximum(mp,jnp.max(sc,axis=1,keepdims=True))
        al=jnp.exp2(mp-m)
        l=ls[h]*al; ps=[]
        for j in range(T//D):
            p=jnp.exp2(sc[:,j*D:(j+1)*D]-m); l=l+p; ps.append(p.astype(BF))
        p=jnp.concatenate(ps,axis=1)
        mx[h]=m; ls[h]=l
        acc[h]=acc[h]*al+jnp.dot(p,vb[s,g],preferred_element_type=F32)
    def wait_recv(s,g):
        for w in range(2): rcopy(w,s,g,partner,fsem.at[0,g,w],rsem.at[s,g,w]).wait_recv()
    def fwd(s,g,w,dc): return rcopy(w,s,g,partner,fsem.at[dc,g,w],rsem.at[s,g,w])
    def shard_step(i,_):
        j=i-core
        dc=jnp.where(j<0,0,j//2+1)
        direct=(j>=0)&(lax.rem(j+2,2)==0)
        s=jnp.where(j<0,partner,(chip-dc)*2+jnp.where(direct,core,1-core))
        for g in range(nkv):
            wait_recv(s,g)
            @pl.when(direct)
            def _():
                for w in range(2): fwd(s,g,w,dc).start()
            for hh in range(grp): head_step(g*grp+hh,s,g)
        return 0
    lax.fori_loop(0,2*chip+core,shard_step,0)
    for h in range(nh):
        o_ref[:,h*D:(h+1)*D]=(acc[h]/jnp.sum(ls[h],axis=1,keepdims=True)).astype(BF)
    for dc in range(n//2):
        @pl.when(send_cond(dc))
        def _(dc=dc):
            for g in range(nkv):
                for w in range(2): my_send(dc,g,w).wait_send()
    for dc in range(1,n//2):
        @pl.when(chip-dc>=0)
        def _(dc=dc):
            s=(chip-dc)*2+core
            for g in range(nkv):
                for w in range(2): fwd(s,g,w,dc).wait_send()
def attn_call(cu,q,kt,v,n=8):
    T,HQ=q.shape; nh=HQ//D; nkv=kt.shape[0]//D
    vm=pl.BlockSpec(memory_space=pltpu.VMEM)
    return pl.pallas_call(functools.partial(attn_body,n,nh,nkv),
        out_shape=jax.ShapeDtypeStruct((T,HQ),BF),
        in_specs=[pl.BlockSpec(memory_space=pltpu.SMEM),vm,vm,vm],
        out_specs=vm,
        scratch_shapes=[pltpu.VMEM((nh,T,2*D),BF),pltpu.VMEM((n,nkv,2*D,T),BF),pltpu.VMEM((n,nkv,T,D),BF),
            pltpu.VMEM((nh,T,D),F32),pltpu.VMEM((nh,T,D),F32),pltpu.VMEM((nh,T,D),F32),
            pltpu.SemaphoreType.DMA((n//2,nkv,2)),pltpu.SemaphoreType.DMA((n,nkv,2)),pltpu.SemaphoreType.DMA((n//2,nkv,2))],
        compiler_params=pltpu.CompilerParams(collective_id=1,has_side_effects=True,vmem_limit_bytes=56*1024*1024),
        cost_estimate=pl.CostEstimate(flops=4*T*T*n*HQ,bytes_accessed=4*T*HQ,transcendentals=T*T*n*nh),
        name="attn")(cu,q,kt,v)

def mlp_body(nsub, h0_ref, at_ref, wo_ref, nm_ref, wg_ref, wu_ref, wd_ref, out_ref, b_scr, acc_scr):
    i=pl.program_id(0)
    @pl.when(i==0)
    def _():
        for r in range(2):
            rows=pl.ds(r*256,256)
            h1=(h0_ref[rows,:].astype(F32)+jnp.dot(at_ref[rows,:],wo_ref[...],preferred_element_type=F32)).astype(BF)
            h1w=h1.astype(F32)
            acc_scr[rows,:]=h1w
            b_scr[rows,:]=(h1w*lax.rsqrt(jnp.mean(h1w*h1w,axis=-1,keepdims=True)+1e-6)*nm_ref[...].astype(F32)).astype(BF)
    b=b_scr[...]
    tf=wg_ref.shape[1]; sub=tf//nsub
    acts=[]
    for j in range(nsub):
        cols=slice(j*sub,(j+1)*sub)
        g=jnp.dot(b,wg_ref[:,cols],preferred_element_type=F32)
        u=jnp.dot(b,wu_ref[:,cols],preferred_element_type=F32)
        acts.append((g*jax.nn.sigmoid(g)*u).astype(BF))
    a=jnp.concatenate(acts,axis=1) if nsub>1 else acts[0]
    acc_scr[...]+=jnp.dot(a,wd_ref[...],preferred_element_type=F32)
    @pl.when(i==pl.num_programs(0)-1)
    def _():
        out_ref[...]=acc_scr[...].astype(BF)
def mlp_call(h0,at,wo,nm,wg,wu,wd,tf=1280,nsub=5):
    T,H=h0.shape; Fd=wg.shape[1]
    full=lambda s: pl.BlockSpec(s,lambda i:(0,)*len(s),pipeline_mode=pl.Buffered(1))
    return pl.pallas_call(functools.partial(mlp_body,nsub),
        out_shape=jax.ShapeDtypeStruct((T,H),BF),
        grid=(Fd//tf,),
        in_specs=[full((T,H)),full((T,H)),full((H,H)),full((1,H)),
                  pl.BlockSpec((H,tf),lambda i:(0,i)),pl.BlockSpec((H,tf),lambda i:(0,i)),pl.BlockSpec((tf,H),lambda i:(i,0))],
        out_specs=pl.BlockSpec((T,H),lambda i:(0,0),pipeline_mode=pl.Buffered(1)),
        scratch_shapes=[pltpu.VMEM((T,H),BF),pltpu.VMEM((T,H),F32)],
        compiler_params=pltpu.CompilerParams(dimension_semantics=("arbitrary",),vmem_limit_bytes=60*1024*1024),
        cost_estimate=pl.CostEstimate(flops=2*T*H*(H+3*Fd),bytes_accessed=2*H*(H+3*Fd),transcendentals=T*Fd),
        name="mlp",
    )(h0,at,wo,nm.reshape(1,H),wg,wu,wd)

HEAD_DIM = 128
NORM_EPS = 1e-6
ROPE_THETA = 1000000.0
MROPE_SPLIT = (16, 40)


def layer_norm(values_in, gain_vec, shift_vec):
    widened = values_in.astype(jnp.float32)
    centered = widened - jnp.mean(widened, axis=-1, keepdims=True)
    spread = jnp.mean(centered * centered, axis=-1, keepdims=True)
    return (centered * lax.rsqrt(spread + NORM_EPS) * gain_vec.astype(jnp.float32) + shift_vec.astype(jnp.float32)).astype(jnp.bfloat16)


def rms_norm(values_in, gain_vec):
    widened = values_in.astype(jnp.float32)
    return (widened * lax.rsqrt(jnp.mean(widened * widened, axis=-1, keepdims=True) + NORM_EPS) * gain_vec.astype(jnp.float32)).astype(jnp.bfloat16)


def merger_mlp(grouped, w_one, b_one, w_two, b_two):
    inner = jax.nn.gelu(jnp.dot(grouped, w_one, preferred_element_type=jnp.float32) + b_one.astype(jnp.float32), approximate=False).astype(jnp.bfloat16)
    return (jnp.dot(inner, w_two, preferred_element_type=jnp.float32) + b_two.astype(jnp.float32)).astype(jnp.bfloat16)


def rope_tables(rope_pos):
    inv_freq = ROPE_THETA ** (-jnp.arange(0, HEAD_DIM, 2, dtype=jnp.float32) / HEAD_DIM)
    freq_idx = jnp.arange(HEAD_DIM // 2)[None, :]
    chosen = jnp.where(freq_idx < MROPE_SPLIT[0], rope_pos[0][:, None], jnp.where(freq_idx < MROPE_SPLIT[1], rope_pos[1][:, None], rope_pos[2][:, None]))
    angles = chosen.astype(jnp.float32) * inv_freq[None, :]
    angles = jnp.concatenate([angles, angles], axis=-1)
    return jnp.cos(angles), jnp.sin(angles)


def apply_rope(heads_in, cos_t, sin_t):
    half_dim = HEAD_DIM // 2
    rotated = jnp.concatenate([-heads_in[..., half_dim:], heads_in[..., :half_dim]], axis=-1)
    return heads_in * cos_t[:, None, :] + rotated * sin_t[:, None, :]


def qkv_project(normed_a, rope_pos, w_q, b_q, w_k, b_k, w_v, b_v):
    tokens = normed_a.shape[0]
    cos_t, sin_t = rope_tables(rope_pos)
    q_lin = jnp.dot(normed_a, w_q, preferred_element_type=jnp.float32) + b_q.astype(jnp.float32)
    k_lin = jnp.dot(normed_a, w_k, preferred_element_type=jnp.float32) + b_k.astype(jnp.float32)
    queries = apply_rope(q_lin.reshape(tokens, -1, HEAD_DIM), cos_t, sin_t).astype(jnp.bfloat16)
    keys_rot = apply_rope(k_lin.reshape(tokens, -1, HEAD_DIM), cos_t, sin_t).astype(jnp.bfloat16)
    values_bf = (jnp.dot(normed_a, w_v, preferred_element_type=jnp.float32) + b_v.astype(jnp.float32)).astype(jnp.bfloat16).reshape(tokens, -1, HEAD_DIM)
    return queries, keys_rot, values_bf


def solution(mesh):
    group_size = mesh.shape['sp']
    row_spec = P(('dp', 'sp'), None)

    def local_step(patches, embeds, dest_slot, rope_pos, cu_doc, ln_w, ln_b, w_one, b_one, w_two, b_two, norm_attn, w_q, b_q, w_k, b_k, w_v, b_v, w_o, norm_mlp, w_gate, w_up, w_down):
        tok_dev = embeds.shape[0]
        merged_dev = dest_slot.shape[0]
        my_shard = lax.axis_index('sp')
        normed = layer_norm(patches, ln_w, ln_b).reshape(merged_dev, -1)
        merged = merger_mlp(normed, w_one, b_one, w_two, b_two)
        to_shard = dest_slot // tok_dev
        send_mask = to_shard[None, :] == jnp.arange(group_size)[:, None]
        send_buf = jnp.where(send_mask[:, :, None], merged[None, :, :], 0)
        received = lax.all_to_all(send_buf, 'sp', 0, 0, tiled=True).reshape(group_size * merged_dev, -1)
        all_slots = lax.all_gather(dest_slot, 'sp', tiled=True)
        pick_mask = all_slots[None, :] == (my_shard * tok_dev + jnp.arange(tok_dev))[:, None]
        placed = jnp.dot(pick_mask.astype(jnp.bfloat16), received, preferred_element_type=jnp.float32).astype(jnp.bfloat16)
        h_zero = jnp.where(jnp.any(pick_mask, axis=1)[:, None], placed, embeds)
        queries, keys_loc, values_loc = qkv_project(rms_norm(h_zero, norm_attn), rope_pos, w_q, b_q, w_k, b_k, w_v, b_v)
        kt_loc = keys_loc.reshape(tok_dev, -1).T
        attn_out = attn_call(cu_doc, queries.reshape(tok_dev, -1), kt_loc, values_loc.reshape(tok_dev, -1), group_size)
        return mlp_call(h_zero, attn_out, w_o, norm_mlp, w_gate, w_up, w_down)

    in_specs = (row_spec, row_spec, P(('dp', 'sp')), P(None, ('dp', 'sp')), P('dp')) + (P(),) * 18
    return jax.shard_map(local_step, mesh=mesh, in_specs=in_specs, out_specs=row_spec, check_vma=False)
```

profile of v0, /device:TPU:7, one launch (start us, length us, event | category | flops | bytes accessed | tf_op | source)
XLA Modules:
  0.0 271.6 jit_solution(17439382132701604686)
XLA Ops:
  0.0 2.3 convert_reduce_fusion
  2.3 2.6 fusion.4
  5.0 0.0 copy-start.3
  5.0 0.0 copy-start.7
  5.0 1.0 fusion.7
  6.0 2.9 %reshape.207 = bf16[256,5120]{1,0:T(8,128)(2,1)} reshape(bf16[1024,1280]{1,0:T(8,128)(2,1)S(1)} %fusion.7) | data formatting | bytes 5242880 | tf_op jit(solution)/shard_map/reshape | solution.py:226
  9.0 37.9 %fusion.58 = bf16[256,1536]{1,0:T(8,128)(2,1)S(1)} fusion(bf16[5120,1536]{1,0:T(8,128)(2,1)} %param.32, f32[1536]{0:T(1024)S(1)} %convert_element_type.73, bf16[256,5120]{1,0:T(8,128)(2,1)} %reshape.207, bf16[5120,5120]{1,0:T(8,128)(2,1)} %param.30, f32[5120]{0:T(1024)S(1)} %convert_element_type.71), kind=kOutput, calls=%fused_computation.73 | convolution fusion | flops 17535598592 | bytes 71591936 | tf_op jit(solution)/shard_map/dot_general | solution.py:189
  46.9 3.2 %broadcast_select_fusion = bf16[8,256,1536]{2,1,0:T(8,128)(2,1)} fusion(pred[8,256]{1,0:T(8,128)(4,1)S(1)} %iota_compare_fusion, bf16[256,1536]{1,0:T(8,128)(2,1)S(1)} %fusion.58), kind=kLoop, calls=%fused_computation.4 | loop fusion | flops 3145728 | bytes 7079936 | tf_op jit(solution)/shard_map/jit(_where)/select_n | solution.py:230
  50.1 3.6 %all-to-all-start = ((bf16[8,256,1536]{2,1,0:T(8,128)(2,1)}), bf16[8,256,1536]{2,1,0:T(8,128)(2,1)}, u32[]{:S(2)}, u32[]{:S(2)}) async-start(bf16[8,256,1536]{2,1,0:T(8,128)(2,1)} %broadcast_select_fusion), calls=%async_computation | async-start | bytes 12582912 | tf_op jit(solution)/shard_map/all_to_all | solution.py:231
  53.8 0.0 copy-start.11
  53.8 0.0 copy-start.12
  53.8 0.1 convert_multiply_fusion.2
  53.9 1.0 fusion.66
  54.9 2.1 mul.145
  57.0 3.5 %copy.32 = f32[512,1536]{1,0:T(8,128)} copy(f32[512,1536]{0,1:T(8,128)} %bitcast.28) | data formatting | bytes 6291456 | tf_op jit(solution)/shard_map/mul | solution.py:204
  60.5 0.6 reshape.211.nm_ref
  61.1 65.9 %all-gather = s32[8,1,256]{2,1,0:T(1,128)S(1)} all-gather(s32[1,1,256]{2,1,0:T(1,128)S(1)} %bitcast.36), channel_id=1, replica_groups=mesh['dp'=1,'sp'=8] {'sp'}, dimensions={0}, use_global_device_ids=true | all-gather | bytes 9216 | tf_op jit(solution)/shard_map/all_gather | solution.py:232
  127.0 0.7 compare_reduce_fusion
  127.6 0.0 slice-start
  127.7 6.6 %fusion.18 = (f32[512]{0:T(512)S(1)}, bf16[512,1536]{1,0:T(8,128)(2,1)S(1)}) fusion(bf16[512,1536]{1,0:T(8,128)(2,1)S(1)} %copy-done.12, bf16[2048,1536]{1,0:T(8,128)(2,1)} %bitcast.2, s32[2048]{0:T(1024)S(1)} %bitcast.32, s32[512]{0:T(512)S(1)} %iota_add_fusion, pred[512]{0:T(512)(128)(4,1)S(1)} %compare_reduce_fusion), kind=kOutput, calls=%fused_computation.35 | convolution fusion | flops 3226205696 | bytes 9449984 | tf_op jit(solution)/shard_map/dot_general | solution.py:234
  134.2 0.8 convolution_add_fusion.4
  135.1 0.1 maximum_multiply_fusion.1
  135.2 0.8 fusion.64
  136.0 4.3 %convolution_add_fusion.1 = f32[512,1536]{1,0:T(8,128)} fusion(bf16[1536,1536]{1,0:T(8,128)(2,1)S(1)} %bitcast.38, f32[1536]{0:T(1024)S(1)} %convert_element_type.79, bf16[512,1536]{1,0:T(8,128)(2,1)S(1)} %get-tuple-element.15.h0_ref, f32[1536]{0:T(1024)S(1)} %convert_element_type.77, f32[512]{0:T(512)S(1)} %add_rsqrt_fusion.1), kind=kOutput, calls=%fused_computation.34 | convolution fusion | flops 2419851264 | bytes 9451520 | tf_op jit(solution)/shard_map/dot_general | solution.py:210
  140.3 3.6 %copy.33 = f32[512,1536]{0,1:T(8,128)} copy(f32[512,1536]{1,0:T(8,128)} %convolution_add_fusion.1) | data formatting | bytes 6291456 | tf_op jit(solution)/shard_map/add | solution.py:210
  143.9 2.4 slice_negate_fusion
  146.3 2.4 maximum_multiply_fusion
  148.7 3.6 %copy.34 = f32[512,1536]{1,0:T(8,128)} copy(f32[512,1536]{0,1:T(8,128)} %bitcast.26) | data formatting | bytes 6291456 | tf_op jit(solution)/shard_map/mul | solution.py:204
  152.2 5.8 %add_convert_fusion.q_ref = bf16[512,1536]{1,0:T(8,128)(2,1)} fusion(f32[512,1536]{1,0:T(8,128)} %copy.34, f32[512,1536]{1,0:T(8,128)} %convolution_add_fusion.1, f32[512,1536]{1,0:T(8,128)} %copy.32), kind=kLoop, calls=%fused_computation.39 | loop fusion | flops 2359296 | bytes 11010048 | tf_op jit(solution)/shard_map/convert_element_type | solution.py:212
  158.1 1.3 fusion.63.v_ref
  159.4 56.1 %attn.1.at_ref = bf16[512,1536]{1,0:T(8,128)(2,1)} custom-call(s32[3]{0:T(128)} %cu_ref.1, bf16[512,1536]{1,0:T(8,128)(2,1)} %add_convert_fusion.q_ref, bf16[256,512]{1,0:T(8,128)(2,1)} %bitcast.30, bf16[512,256]{1,0:T(8,128)(2,1)} %fusion.63.v_ref), custom_call_target="tpu_custom_call" | custom-call | flops 12884901888 | bytes 3145728 | tf_op jit(solution)/shard_map/attn/pallas_call | solution.py:120
  215.5 56.1 %mlp.1 = bf16[512,1536]{1,0:T(8,128)(2,1)} custom-call(bf16[512,1536]{1,0:T(8,128)(2,1)} %copy-done.16, bf16[512,1536]{1,0:T(8,128)(2,1)} %attn.1.at_ref, bf16[1536,1536]{1,0:T(8,128)(2,1)} %wo_ref.1, bf16[1,1536]{1,0:T(2,128)(2,1)} %reshape.211.nm_ref, bf16[1536,8960]{1,0:T(8,128)(2,1)} %wg_ref.1, bf16[1536,8960]{1,0:T(8,128)(2,1)} %wu_ref.1, ...), custom_call_target="tpu_custom_call" | custom-call | flops 44694503424 | bytes 87293952 | tf_op jit(solution)/shard_map/mlp/pallas_call | solution.py:157
  (55 shorter events, 0.2 us)
Async XLA Ops:
  0.0 134.2 %copy-start = (bf16[1536,256]{1,0:T(8,128)(2,1)S(1)}, bf16[1536,256]{1,0:T(8,128)(2,1)}, u32[]{:S(2)}) copy-start(bf16[1536,256]{1,0:T(8,128)(2,1)} %param.37) | copy-start | bytes 2359300
  0.0 5.0 %copy-start.2 = (bf16[1024,1280]{1,0:T(8,128)(2,1)S(1)}, bf16[1024,1280]{1,0:T(8,128)(2,1)}, u32[]{:S(2)}) copy-start(bf16[1024,1280]{1,0:T(8,128)(2,1)} %param.23) | copy-start | bytes 7864324
  0.0 4.9 %copy-start.5 = (bf16[1280]{0:T(1024)(128)(2,1)S(1)}, bf16[1280]{0:T(1024)(128)(2,1)}, u32[]{:S(2)}) copy-start(bf16[1280]{0:T(1024)(128)(2,1)} %param.28) | copy-start | bytes 7684
  0.0 4.9 %copy-start.6 = (bf16[1280]{0:T(1024)(128)(2,1)S(1)}, bf16[1280]{0:T(1024)(128)(2,1)}, u32[]{:S(2)}) copy-start(bf16[1280]{0:T(1024)(128)(2,1)} %param.29) | copy-start | bytes 7684
  5.0 4.0 %copy-start.3 = (bf16[5120]{0:T(1024)(128)(2,1)S(1)}, bf16[5120]{0:T(1024)(128)(2,1)}, u32[]{:S(2)}) copy-start(bf16[5120]{0:T(1024)(128)(2,1)} %param.31) | copy-start | bytes 30724
  5.0 4.0 %copy-start.7 = (bf16[1536]{0:T(1024)(128)(2,1)S(1)}, bf16[1536]{0:T(1024)(128)(2,1)}, u32[]{:S(2)}) copy-start(bf16[1536]{0:T(1024)(128)(2,1)} %param.33) | copy-start | bytes 9220
  5.0 4.0 %copy-start.10 = (s32[256]{0:T(256)S(1)}, s32[256]{0:T(256)}, u32[]{:S(2)}) copy-start(s32[256]{0:T(256)} %param.25) | copy-start | bytes 3076
  50.1 3.6 %copy-start.8 = (bf16[1536]{0:T(1024)(128)(2,1)S(1)}, bf16[1536]{0:T(1024)(128)(2,1)}, u32[]{:S(2)}) copy-start(bf16[1536]{0:T(1024)(128)(2,1)} %param.34) | copy-start | bytes 9220
  50.1 3.6 %copy-start.14 = (bf16[256]{0:T(256)(128)(2,1)S(1)}, bf16[256]{0:T(256)(128)(2,1)}, u32[]{:S(2)}) copy-start(bf16[256]{0:T(256)(128)(2,1)} %param.38) | copy-start | bytes 1540
  50.1 3.7 %copy-start.9 = (bf16[1536]{0:T(1024)(128)(2,1)S(1)}, bf16[1536]{0:T(1024)(128)(2,1)}, u32[]{:S(2)}) copy-start(bf16[1536]{0:T(1024)(128)(2,1)} %param.36) | copy-start | bytes 9220
  50.1 3.7 %copy-start.4 = (s32[3,512]{1,0:T(4,128)S(1)}, s32[3,512]{1,0:T(4,128)}, u32[]{:S(2)}) copy-start(s32[3,512]{1,0:T(4,128)} %param.26) | copy-start | bytes 18436
  50.1 77.5 %all-to-all-start = ((bf16[8,256,1536]{2,1,0:T(8,128)(2,1)}), bf16[8,256,1536]{2,1,0:T(8,128)(2,1)}, u32[]{:S(2)}, u32[]{:S(2)}) async-start(bf16[8,256,1536]{2,1,0:T(8,128)(2,1)} %broadcast_select_fusion), calls=%async_computation | async-start | bytes 12582912 | tf_op jit(solution)/shard_map/all_to_all | solution.py:231
  53.8 6.7 %copy-start.15 = (bf16[256]{0:T(256)(128)(2,1)S(1)}, bf16[256]{0:T(256)(128)(2,1)}, u32[]{:S(2)}) copy-start(bf16[256]{0:T(256)(128)(2,1)} %param.40) | copy-start | bytes 1540
  53.8 6.7 %copy-start.11 = (bf16[1536]{0:T(1024)(128)(2,1)S(1)}, bf16[1536]{0:T(1024)(128)(2,1)}, u32[]{:S(2)}) copy-start(bf16[1536]{0:T(1024)(128)(2,1)} %param.42) | copy-start | bytes 9220
  53.8 73.8 %copy-start.12 = (bf16[512,1536]{1,0:T(8,128)(2,1)S(1)}, bf16[512,1536]{1,0:T(8,128)(2,1)}, u32[]{:S(2)}) copy-start(bf16[512,1536]{1,0:T(8,128)(2,1)} %param.24) | copy-start | bytes 4718596
  127.6 8.4 %slice-start = ((s8[4718592]{0:T(1024)(128)(4,1)}), s8[4194304]{0:T(1024)(128)(4,1)S(1)}, s32[]{:S(2)}) async-start(s8[4718592]{0:T(1024)(128)(4,1)} %bitcast.37), calls=%async_computation.1 | async-start | bytes 8388608
  127.7 8.3 %slice-start.1 = ((s8[4718592]{0:T(1024)(128)(4,1)}), s8[524288]{0:T(1024)(128)(4,1)S(1)}, s32[]{:S(2)}) async-start(s8[4718592]{0:T(1024)(128)(4,1)} %bitcast.37), calls=%async_computation.2 | async-start | bytes 1048576
  134.2 1.8 copy-start.16
  152.2 5.8 %copy-start.13 = (bf16[1536,256]{1,0:T(8,128)(2,1)S(1)}, bf16[1536,256]{1,0:T(8,128)(2,1)}, u32[]{:S(2)}) copy-start(bf16[1536,256]{1,0:T(8,128)(2,1)} %param.39) | copy-start | bytes 2359300
  152.2 5.8 %copy-start.17 = (bf16[512,1536]{1,0:T(8,128)(2,1)S(1)}, bf16[512,1536]{1,0:T(8,128)(2,1)}, u32[]{:S(2)}) copy-start(bf16[512,1536]{1,0:T(8,128)(2,1)} %copy-done.16) | copy-start | bytes 4718596
  215.5 56.2 %copy-start.1 = (bf16[1536,256]{1,0:T(8,128)(2,1)S(1)}, bf16[1536,256]{1,0:T(8,128)(2,1)}, u32[]{:S(2)}) copy-start(bf16[1536,256]{1,0:T(8,128)(2,1)} %param.37) | copy-start | bytes 2359300
where the time goes:
time: 272 us
  Pallas kernels  112 us (41%)
  blocking collectives  65.9 us (24%)
  matrix products  50.8 us (19%)
  other arithmetic  22.4 us (8%)
  local copies, waits for them, and re-layouts  16.3 us (6%)
  starting transfers between devices  3.59 us (1%)
    all_gather x1, blocking collectives, local_step(): all_slots = lax.all_gather(dest_slot, 'sp', tiled=True)  65.9 us
    pallas_call x1, Pallas kernels, mlp_call(): pl.pallas_call(functools.partial(mlp_body, nsub), out_shape=jax.ShapeDtyp...  56.1 us
    pallas_call x1, Pallas kernels, attn_call(): pl.pallas_call(functools.partial(attn_body, n, nh, nkv), out_shape=jax.Sh...  56.1 us
    dot_general x1, matrix products, merger_mlp(): jnp.dot(inner, w_two, preferred_element_type=jnp.float32)  37.9 us
    mul x3, local copies, waits for them, and re-layouts, apply_rope(): return heads_in * cos_t[:, None, :] + rotated * sin_t[:, None, :]  9.15 us
    dot_general x1, matrix products, local_step(): jnp.dot(pick_mask.astype(jnp.bfloat16), received, preferred_element_type=...  6.55 us
    convert_element_type x1, other arithmetic, qkv_project(): apply_rope(q_lin.reshape(tokens, -1, HEAD_DIM), cos_t, sin_t)  5.83 us
  transfers between devices with their start and end apart: 1, of which 0 were waited for; matrix products, arithmetic and copies ran while one was open for 3% of the time, Pallas kernels for 0%

commit v1 on v0

--- a/solution.py
+++ b/solution.py
@@ -8,8 +8,8 @@
 
 BF = jnp.bfloat16
 F32 = jnp.float32
-MESH=pl.DeviceIdType.MESH
-D=128
+MESH = pl.DeviceIdType.MESH
+D = 128
 SC=D**-0.5*1.4426950408889634
 def attn_body(n, nh, nkv, cu_ref, q_ref, kt_ref, v_ref, o_ref, qa, kb, vb, acc, mx, ls, ssem, rsem, fsem):
     T=q_ref.shape[0]; grp=nh//nkv
@@ -127,7 +127,153 @@
         compiler_params=pltpu.CompilerParams(collective_id=1,has_side_effects=True,vmem_limit_bytes=56*1024*1024),
         cost_estimate=pl.CostEstimate(flops=4*T*T*n*HQ,bytes_accessed=4*T*HQ,transcendentals=T*T*n*nh),
         name="attn")(cu,q,kt,v)
-
+TW=256
+NB=5
+def front_body(n, pat_ref, emb_ref, slot_ref, cos_ref, sin_ref, lw_ref, lb_ref, w1_ref, b1_ref, w2_ref, b2_ref, na_ref, wq_ref, bq_ref, wk_ref, bk_ref, wv_ref, bv_ref,
+               h0_ref, q_ref, kt_ref, v_ref,
+               zf, z, inner, wbuf, mbuf, slots, onehot, hacc, wq, wk, wv,
+               wsem, qsem, slot_s, slot_r, own_s, fwd_s, rsem):
+    R=mbuf.shape[1]; T=emb_ref.shape[0]; V=pat_ref.shape[1]; K1=w1_ref.shape[0]; H=w2_ref.shape[1]
+    n1=w1_ref.shape[1]//TW; n2=H//TW
+    me=lax.axis_index('sp'); chip=me//2; core=lax.rem(me,2)
+    partner=chip*2+1-core
+    cx=lax.rem(chip,2); cy=chip//2
+    xn=(cy*2+1-cx)*2+core; yn=((1-cy)*2+cx)*2+core; dg=((1-cy)*2+1-cx)*2+core
+    other=lambda i: i+1-2*core
+    dev=lambda i: {'sp':i}
+    bar=pltpu.get_barrier_semaphore()
+    for d in range(1,n):
+        pl.semaphore_signal(bar,inc=1,device_id=dev(lax.rem(me+d,n)),device_id_type=MESH)
+    def w1copy(t,s): return pltpu.make_async_copy(w1_ref.at[:,pl.ds(pl.multiple_of(t*TW,TW),TW)],wbuf.at[s],wsem.at[s])
+    def w2copy(t,s): return pltpu.make_async_copy(w2_ref.at[:,pl.ds(pl.multiple_of(t*TW,TW),TW)],wbuf.at[s],wsem.at[s])
+    for t in range(NB): w1copy(t,t).start()
+    CH=128
+    def ln(i,_):
+        x=pat_ref[pl.ds(pl.multiple_of(i*CH,CH),CH),:].astype(F32)
+        c=x-jnp.mean(x,axis=-1,keepdims=True)
+        var=jnp.mean(c*c,axis=-1,keepdims=True)
+        y=c*lax.rsqrt(var+1e-6)*lw_ref[...].astype(F32)+lb_ref[...].astype(F32)
+        for p in range(V//D): zf[p]=y[:,p*D:(p+1)*D]
+        for j in range(4):
+            for p in range(V//D):
+                z[pl.ds(pl.multiple_of(i*(CH//4),CH//4),CH//4),j*V+p*D:j*V+(p+1)*D]=zf[p,pl.ds(j,CH//4,stride=4),:].astype(BF)
+        return 0
+    lax.fori_loop(0,pat_ref.shape[0]//CH,ln,0)
+    pl.semaphore_wait(bar,n-1)
+    def slot_copy(d):
+        return pltpu.make_async_remote_copy(src_ref=slot_ref,dst_ref=slots.at[me],send_sem=slot_s.at[d-1],recv_sem=slot_r.at[me],device_id=dev(lax.rem(me+d,n)),device_id_type=MESH)
+    for d in range(1,n): slot_copy(d).start()
+    slots[me]=slot_ref[...]
+    def first(i,_):
+        s=lax.rem(i,NB)
+        w1copy(i,s).wait()
+        y=jnp.dot(z[...],wbuf[s],preferred_element_type=F32)
+        cols=pl.ds(pl.multiple_of(i*TW,TW),TW)
+        y=y+b1_ref[:,cols].astype(F32)
+        inner[:,cols]=(0.5*y*(1.0+lax.erf(y*0.7071067811865476))).astype(BF)
+        @pl.when(i+NB<n1)
+        def _(): w1copy(i+NB,s).start()
+        @pl.when(i+NB>=n1)
+        def _(): w2copy(i+NB-n1,s).start()
+        return 0
+    lax.fori_loop(0,n1,first,0)
+    qc=pltpu.make_async_copy(wq_ref,wq,qsem.at[0]); kc=pltpu.make_async_copy(wk_ref,wk,qsem.at[1]); vc=pltpu.make_async_copy(wv_ref,wv,qsem.at[2])
+    def tile(s,j): return mbuf.at[s,:,pl.ds(j*TW,TW)]
+    def send(src,j,tgt,ss):
+        return pltpu.make_async_remote_copy(src_ref=tile(src,j),dst_ref=tile(src,j),send_sem=ss,recv_sem=rsem.at[src,j],device_id=dev(tgt),device_id_type=MESH)
+    for j in range(n2):
+        t=n1+j; s=t%NB
+        w2copy(j,s).wait()
+        y=jnp.dot(inner[...],wbuf[s],preferred_element_type=F32)+b2_ref[:,j*TW:(j+1)*TW].astype(F32)
+        mbuf[me,:,j*TW:(j+1)*TW]=y.astype(BF)
+        for a,tgt in enumerate((xn,yn,partner)): send(me,j,tgt,own_s.at[a,j]).start()
+        if t+NB<n1+n2: w2copy(j+NB,s).start()
+        elif t+NB==n1+n2: qc.start(); kc.start(); vc.start()
+    for d in range(1,n):
+        s=lax.rem(me+d,n)
+        pltpu.make_async_remote_copy(src_ref=slot_ref,dst_ref=slots.at[s],send_sem=slot_s.at[0],recv_sem=slot_r.at[s],device_id=dev(s),device_id_type=MESH).wait_recv()
+    base=me*T
+    def oh(s,_):
+        sl=slots[s][0:1,:]
+        tok=lax.broadcasted_iota(jnp.int32,(T,R),0)+base
+        onehot[s]=jnp.where(tok==sl,1.0,0.0).astype(BF)
+        return 0
+    lax.fori_loop(0,n,oh,0)
+    def place(s,j,firsttime=False):
+        c=slice(j*TW,(j+1)*TW)
+        p=jnp.dot(onehot[s],mbuf[s,:,c],preferred_element_type=F32)
+        if firsttime: hacc[:,c]=p
+        else: hacc[:,c]+=p
+    for j in range(n2): place(me,j,True)
+    def arrive(s,j): send(s,j,partner,own_s.at[0,0]).wait_recv()
+    fw=[]
+    def forward(s,j,tgt,kind):
+        c=send(s,j,tgt,fwd_s.at[kind,j]); c.start(); fw.append(c)
+    for j in range(n2):
+        arrive(xn,j)
+        if j%2==0: forward(xn,j,yn,0)
+        forward(xn,j,partner,1)
+        arrive(yn,j)
+        if j%2==1: forward(yn,j,xn,0)
+        forward(yn,j,partner,2)
+        arrive(partner,j)
+        place(xn,j); place(yn,j); place(partner,j)
+        if j>0:
+            for s in (other(xn),other(yn)):
+                arrive(s,j-1); place(s,j-1)
+    for s in (other(xn),other(yn)):
+        arrive(s,n2-1); place(s,n2-1)
+    for j in range(n2):
+        arrive(dg,j); forward(dg,j,partner,3); place(dg,j)
+        if j>0: arrive(other(dg),j-1); place(other(dg),j-1)
+    arrive(other(dg),n2-1); place(other(dg),n2-1)
+    hit=onehot[0].astype(F32)
+    for s in range(1,n): hit=hit+onehot[s].astype(F32)
+    has=jnp.sum(hit,axis=1,keepdims=True)>0.5
+    h0=jnp.where(has,hacc[...],emb_ref[...].astype(F32))
+    h0_ref[...]=h0.astype(BF)
+    a=(h0*lax.rsqrt(jnp.mean(h0*h0,axis=-1,keepdims=True)+1e-6)*na_ref[...].astype(F32)).astype(BF)
+    qc.wait(); kc.wait(); vc.wait()
+    def rope(x):
+        return x*cos_ref[...]+pltpu.roll(x,D//2,1)*sin_ref[...]
+    for i in range(H//TW):
+        y=jnp.dot(a,wq[:,i*TW:(i+1)*TW],preferred_element_type=F32)+bq_ref[:,i*TW:(i+1)*TW].astype(F32)
+        for h in range(TW//D):
+            q_ref[:,i*TW+h*D:i*TW+(h+1)*D]=rope(y[:,h*D:(h+1)*D]).astype(BF)
+    y=jnp.dot(a,wk[...],preferred_element_type=F32)+bk_ref[...].astype(F32)
+    for h in range(wk.shape[1]//D):
+        kt_ref[h*D:(h+1)*D,:]=rope(y[:,h*D:(h+1)*D]).T.astype(BF)
+    v_ref[...]=(jnp.dot(a,wv[...],preferred_element_type=F32)+bv_ref[...].astype(F32)).astype(BF)
+    for d in range(1,n): slot_copy(d).wait_send()
+    for j in range(n2):
+        for a_,tgt in enumerate((xn,yn,partner)): send(me,j,tgt,own_s.at[a_,j]).wait_send()
+    for c in fw: c.wait_send()
+def rope_tables(rope_pos):
+    inv_freq = 1000000.0 ** (-jnp.arange(0, 128, 2, dtype=jnp.float32) / 128)
+    fi = jnp.arange(64)[None, :]
+    chosen = jnp.where(fi < 16, rope_pos[0][:, None], jnp.where(fi < 40, rope_pos[1][:, None], rope_pos[2][:, None]))
+    ang = chosen.astype(jnp.float32) * inv_freq[None, :]
+    c, s = jnp.cos(ang), jnp.sin(ang)
+    return jnp.concatenate([c, c], axis=-1), jnp.concatenate([-s, s], axis=-1)
+def front_call(pat,emb,slot,rope_pos,lw,lb,w1,b1,w2,b2,na,wq,bq,wk,bk,wv,bv,n=8):
+    T,H=emb.shape; R=slot.shape[0]; K1=w1.shape[0]; V=pat.shape[1]; KV=wk.shape[1]
+    cos,sin=rope_tables(rope_pos)
+    slot8=jnp.broadcast_to(slot[None,:],(8,R))
+    vm=pl.BlockSpec(memory_space=pltpu.VMEM); hbm=pl.BlockSpec(memory_space=pl.ANY)
+    r1=lambda x: x.reshape(1,-1)
+    n2=H//TW
+    DS=pltpu.SemaphoreType.DMA
+    return pl.pallas_call(functools.partial(front_body,n),
+        out_shape=(jax.ShapeDtypeStruct((T,H),BF),jax.ShapeDtypeStruct((T,wq.shape[1]),BF),jax.ShapeDtypeStruct((KV,T),BF),jax.ShapeDtypeStruct((T,KV),BF)),
+        in_specs=[vm,vm,vm,vm,vm,vm,vm,hbm,vm,hbm,vm,vm,hbm,vm,hbm,vm,hbm,vm],
+        out_specs=(vm,)*4,
+        scratch_shapes=[pltpu.VMEM((V//D,128,D),F32),pltpu.VMEM((R,K1),BF),pltpu.VMEM((R,w1.shape[1]),BF),pltpu.VMEM((NB,K1,TW),BF),
+            pltpu.VMEM((n,R,H),BF),pltpu.VMEM((n,8,R),jnp.int32),pltpu.VMEM((n,T,R),BF),pltpu.VMEM((T,H),F32),
+            pltpu.VMEM(wq.shape,BF),pltpu.VMEM(wk.shape,BF),pltpu.VMEM(wv.shape,BF),
+            DS((NB,)),DS((3,)),DS((n-1,)),DS((n,)),DS((3,n2)),DS((4,n2)),DS((n,n2))],
+        compiler_params=pltpu.CompilerParams(collective_id=2,has_side_effects=True,vmem_limit_bytes=62*1024*1024),
+        cost_estimate=pl.CostEstimate(flops=2*R*K1*(K1+H),bytes_accessed=2*K1*(K1+H),transcendentals=R*K1),
+        name="front")(pat,emb,slot8,cos,sin,r1(lw),r1(lb),w1,r1(b1),w2,r1(b2),r1(na),wq,r1(bq),wk,r1(bk),wv,r1(bv))
 def mlp_body(nsub, h0_ref, at_ref, wo_ref, nm_ref, wg_ref, wu_ref, wd_ref, out_ref, b_scr, acc_scr):
     i=pl.program_id(0)
     @pl.when(i==0)
@@ -166,76 +312,14 @@
         name="mlp",
     )(h0,at,wo,nm.reshape(1,H),wg,wu,wd)
 
-HEAD_DIM = 128
-NORM_EPS = 1e-6
-ROPE_THETA = 1000000.0
-MROPE_SPLIT = (16, 40)
-
-
-def layer_norm(values_in, gain_vec, shift_vec):
-    widened = values_in.astype(jnp.float32)
-    centered = widened - jnp.mean(widened, axis=-1, keepdims=True)
-    spread = jnp.mean(centered * centered, axis=-1, keepdims=True)
-    return (centered * lax.rsqrt(spread + NORM_EPS) * gain_vec.astype(jnp.float32) + shift_vec.astype(jnp.float32)).astype(jnp.bfloat16)
-
-
-def rms_norm(values_in, gain_vec):
-    widened = values_in.astype(jnp.float32)
-    return (widened * lax.rsqrt(jnp.mean(widened * widened, axis=-1, keepdims=True) + NORM_EPS) * gain_vec.astype(jnp.float32)).astype(jnp.bfloat16)
-
-
-def merger_mlp(grouped, w_one, b_one, w_two, b_two):
-    inner = jax.nn.gelu(jnp.dot(grouped, w_one, preferred_element_type=jnp.float32) + b_one.astype(jnp.float32), approximate=False).astype(jnp.bfloat16)
-    return (jnp.dot(inner, w_two, preferred_element_type=jnp.float32) + b_two.astype(jnp.float32)).astype(jnp.bfloat16)
-
-
-def rope_tables(rope_pos):
-    inv_freq = ROPE_THETA ** (-jnp.arange(0, HEAD_DIM, 2, dtype=jnp.float32) / HEAD_DIM)
-    freq_idx = jnp.arange(HEAD_DIM // 2)[None, :]
-    chosen = jnp.where(freq_idx < MROPE_SPLIT[0], rope_pos[0][:, None], jnp.where(freq_idx < MROPE_SPLIT[1], rope_pos[1][:, None], rope_pos[2][:, None]))
-    angles = chosen.astype(jnp.float32) * inv_freq[None, :]
-    angles = jnp.concatenate([angles, angles], axis=-1)
-    return jnp.cos(angles), jnp.sin(angles)
-
-
-def apply_rope(heads_in, cos_t, sin_t):
-    half_dim = HEAD_DIM // 2
-    rotated = jnp.concatenate([-heads_in[..., half_dim:], heads_in[..., :half_dim]], axis=-1)
-    return heads_in * cos_t[:, None, :] + rotated * sin_t[:, None, :]
-
-
-def qkv_project(normed_a, rope_pos, w_q, b_q, w_k, b_k, w_v, b_v):
-    tokens = normed_a.shape[0]
-    cos_t, sin_t = rope_tables(rope_pos)
-    q_lin = jnp.dot(normed_a, w_q, preferred_element_type=jnp.float32) + b_q.astype(jnp.float32)
-    k_lin = jnp.dot(normed_a, w_k, preferred_element_type=jnp.float32) + b_k.astype(jnp.float32)
-    queries = apply_rope(q_lin.reshape(tokens, -1, HEAD_DIM), cos_t, sin_t).astype(jnp.bfloat16)
-    keys_rot = apply_rope(k_lin.reshape(tokens, -1, HEAD_DIM), cos_t, sin_t).astype(jnp.bfloat16)
-    values_bf = (jnp.dot(normed_a, w_v, preferred_element_type=jnp.float32) + b_v.astype(jnp.float32)).astype(jnp.bfloat16).reshape(tokens, -1, HEAD_DIM)
-    return queries, keys_rot, values_bf
-
 
 def solution(mesh):
     group_size = mesh.shape['sp']
     row_spec = P(('dp', 'sp'), None)
 
     def local_step(patches, embeds, dest_slot, rope_pos, cu_doc, ln_w, ln_b, w_one, b_one, w_two, b_two, norm_attn, w_q, b_q, w_k, b_k, w_v, b_v, w_o, norm_mlp, w_gate, w_up, w_down):
-        tok_dev = embeds.shape[0]
-        merged_dev = dest_slot.shape[0]
-        my_shard = lax.axis_index('sp')
-        normed = layer_norm(patches, ln_w, ln_b).reshape(merged_dev, -1)
-        merged = merger_mlp(normed, w_one, b_one, w_two, b_two)
-        to_shard = dest_slot // tok_dev
-        send_mask = to_shard[None, :] == jnp.arange(group_size)[:, None]
-        send_buf = jnp.where(send_mask[:, :, None], merged[None, :, :], 0)
-        received = lax.all_to_all(send_buf, 'sp', 0, 0, tiled=True).reshape(group_size * merged_dev, -1)
-        all_slots = lax.all_gather(dest_slot, 'sp', tiled=True)
-        pick_mask = all_slots[None, :] == (my_shard * tok_dev + jnp.arange(tok_dev))[:, None]
-        placed = jnp.dot(pick_mask.astype(jnp.bfloat16), received, preferred_element_type=jnp.float32).astype(jnp.bfloat16)
-        h_zero = jnp.where(jnp.any(pick_mask, axis=1)[:, None], placed, embeds)
-        queries, keys_loc, values_loc = qkv_project(rms_norm(h_zero, norm_attn), rope_pos, w_q, b_q, w_k, b_k, w_v, b_v)
-        kt_loc = keys_loc.reshape(tok_dev, -1).T
-        attn_out = attn_call(cu_doc, queries.reshape(tok_dev, -1), kt_loc, values_loc.reshape(tok_dev, -1), group_size)
+        h_zero, q, k, v = front_call(patches, embeds, dest_slot, rope_pos, ln_w, ln_b, w_one, b_one, w_two, b_two, norm_attn, w_q, b_q, w_k, b_k, w_v, b_v, group_size)
+        attn_out = attn_call(cu_doc, q, k, v, group_size)
         return mlp_call(h_zero, attn_out, w_o, norm_mlp, w_gate, w_up, w_down)
 
     in_specs = (row_spec, row_spec, P(('dp', 'sp')), P(None, ('dp', 'sp')), P('dp')) + (P(),) * 18

time: 272 us -> 187 us (0.69)
  blocking collectives: 65.9 us -> 0 us
  Pallas kernels: 112 us -> 171 us
  matrix products: 50.8 us -> 0 us
  other arithmetic: 22.4 us -> 2.75 us
  starting transfers between devices: 3.59 us -> 0 us
  local copies, waits for them, and re-layouts: 16.3 us -> 12.9 us
    all_gather x1 -> x0, blocking collectives: 65.9 us -> none  [local_step(): all_slots = lax.all_gather(dest_slot, 'sp', tiled=True)]
    pallas_call x0 -> x1, Pallas kernels: none -> 60 us  [front_call(): pl.pallas_call(functools.partial(front_body, n), out_shape=(jax.ShapeDtyp...]
    dot_general x5 -> x0, matrix products: 50.8 us -> none  [the longest x1 37.9 us: merger_mlp(): jnp.dot(inner, w_two, preferred_element_type=jnp.float32)]
    mul x3 -> x0, local copies, waits for them, and re-layouts: 9.15 us -> none  [apply_rope(): return heads_in * cos_t[:, None, :] + rotated * sin_t[:, None, :]]
    convert_element_type x11 -> x0, other arithmetic: 7.73 us -> none  [the longest x1 5.83 us: qkv_project(): apply_rope(q_lin.reshape(tokens, -1, HEAD_DIM), cos_t, sin_t)]
    reshape x1 -> x8, local copies, waits for them, and re-layouts: 2.92 us -> 10.2 us  [front_call(): r1 = lambda x: x.reshape(1, -1)]
    reduce_sum x2 -> x0, other arithmetic: 4.86 us -> none  [the longest x1 2.56 us: layer_norm(): spread = jnp.mean(centered * centered, axis=-1, keepdims=True)]
    all_to_all x1 -> x0, starting transfers between devices: 3.59 us -> none  [local_step(): lax.all_to_all(send_buf, 'sp', 0, 0, tiled=True)]
  transfers between devices with their start and end apart: 1 -> 0, of which waited for: 0 -> 0; matrix products, arithmetic and copies ran while one was open for 3% -> 0% of each run, Pallas kernels for 0% -> 0%
where the time goes in v1:
time: 187 us
  Pallas kernels  171 us (91%)
  local copies, waits for them, and re-layouts  12.9 us (7%)
  other arithmetic  2.75 us (1%)
    pallas_call x1, Pallas kernels, front_call(): pl.pallas_call(functools.partial(front_body, n), out_shape=(jax.ShapeDtyp...  60 us
    pallas_call x1, Pallas kernels, mlp_call(): pl.pallas_call(functools.partial(mlp_body, nsub), out_shape=jax.ShapeDtyp...  56.1 us
    pallas_call x1, Pallas kernels, attn_call(): pl.pallas_call(functools.partial(attn_body, n, nh, nkv), out_shape=jax.Sh...  54.8 us
    reshape x8, local copies, waits for them, and re-layouts, front_call(): r1 = lambda x: x.reshape(1, -1)  10.2 us

profile of v1, /device:TPU:7, one launch (start us, length us, event | category | flops | bytes accessed | tf_op | source)
XLA Modules:
  0.0 186.6 jit_solution(14720343459568090000)
XLA Ops:
  0.0 1.3 broadcast_in_dim.54.slot_ref
  1.3 0.8 fusion.3
  2.1 1.7 fusion.2
  3.9 1.0 pad_maximum_fusion
  4.9 1.3 reshape.48.lw_ref
  6.1 1.3 reshape.49.lb_ref
  7.4 1.3 reshape.50.b1_ref
  8.7 1.3 reshape.51.b2_ref
  10.0 1.3 reshape.52.na_ref
  11.3 1.3 reshape.53.bq_ref
  12.6 1.2 reshape.54.bk_ref
  13.8 1.2 reshape.55.bv_ref
  15.1 60.0 %front.1 = (bf16[512,1536]{1,0:T(8,128)(2,1)}, bf16[512,1536]{1,0:T(8,128)(2,1)}, bf16[256,512]{1,0:T(8,128)(2,1)}, bf16[512,256]{1,0:T(8,128)(2,1)}) custom-call(bf16[1024,1280]{1,0:T(8,128)(2,1)} %pat_ref.1, bf16[512,1536]{1,0:T(8,128)(2,1)} %emb_ref.1, s32[8,256]{1,0:T(8,128)} %broadcast_in_dim.54.slot_ref, f32[512,128]{1,0:T(8,128)} %get-tuple-element.19.cos_ref, ...), custom_call_target="tpu_custom_call" | custom-call | flops 17448304640 | bytes 68157440 | tf_op jit(solution)/shard_map/front/pallas_call | solution.py:266
  75.1 0.0 copy-start
  75.1 54.8 %attn.1.at_ref = bf16[512,1536]{1,0:T(8,128)(2,1)} custom-call(s32[3]{0:T(128)} %cu_ref.1, bf16[512,1536]{1,0:T(8,128)(2,1)} %get-tuple-element.10.q_ref, bf16[256,512]{1,0:T(8,128)(2,1)} %get-tuple-element.11.kt_ref, bf16[512,256]{1,0:T(8,128)(2,1)} %get-tuple-element.12.v_ref), custom_call_target="tpu_custom_call" | custom-call | flops 12884901888 | bytes 3145728 | tf_op jit(solution)/shard_map/attn/pallas_call | solution.py:120
  129.9 0.0 copy-done
  129.9 0.6 reshape.56.nm_ref
  130.5 56.1 %mlp.1 = bf16[512,1536]{1,0:T(8,128)(2,1)} custom-call(bf16[512,1536]{1,0:T(8,128)(2,1)} %get-tuple-element.9.h0_ref, bf16[512,1536]{1,0:T(8,128)(2,1)} %attn.1.at_ref, bf16[1536,1536]{1,0:T(8,128)(2,1)} %wo_ref.1, bf16[1,1536]{1,0:T(2,128)(2,1)} %reshape.56.nm_ref, bf16[1536,8960]{1,0:T(8,128)(2,1)} %wg_ref.1, bf16[1536,8960]{1,0:T(8,128)(2,1)} %wu_ref.1, ...), custom_call_target="tpu_custom_call" | custom-call | flops 44694503424 | bytes 87293952 | tf_op jit(solution)/shard_map/mlp/pallas_call | solution.py:303
  (3 shorter events, 0.0 us)
Async XLA Ops:
  75.1 54.8 %copy-start = (bf16[1536]{0:T(1024)(128)(2,1)S(1)}, bf16[1536]{0:T(1024)(128)(2,1)}, u32[]{:S(2)}) copy-start(bf16[1536]{0:T(1024)(128)(2,1)} %param.42) | copy-start | bytes 9220

commit v2 on v1

--- a/solution.py
+++ b/solution.py
@@ -11,7 +11,7 @@
 MESH = pl.DeviceIdType.MESH
 D = 128
 SC=D**-0.5*1.4426950408889634
-def attn_body(n, nh, nkv, cu_ref, q_ref, kt_ref, v_ref, o_ref, qa, kb, vb, acc, mx, ls, ssem, rsem, fsem):
+def attn_body(n, nh, nkv, cu_ref, q_ref, kt_ref, v_ref, o_ref, qa, kb, vb, acc, mx, ls, sb, pb, ssem, rsem, fsem):
     T=q_ref.shape[0]; grp=nh//nkv
     ncut=cu_ref.shape[0]-2
     me=lax.axis_index('sp'); chip=me//2; core=lax.rem(me,2); partner=chip*2+1-core
@@ -74,16 +74,17 @@
             acc[h,rows,:]=jnp.dot(p.astype(BF),vg,preferred_element_type=F32)
         return 0
     lax.fori_loop(0,nh,own,0)
-    def head_step(h,s,g):
-        sc=jnp.dot(qa[h],kb[s,g],preferred_element_type=F32)*SC
+    def qk(h,s,g): return jnp.dot(qa[h],kb[s,g],preferred_element_type=F32)
+    def soft(h,sc):
         mp=mx[h]
-        m=jnp.maximum(mp,jnp.max(sc,axis=1,keepdims=True))
+        m=jnp.maximum(mp,jnp.max(sc,axis=1,keepdims=True)*SC)
         al=jnp.exp2(mp-m)
         l=ls[h]*al; ps=[]
         for j in range(T//D):
-            p=jnp.exp2(sc[:,j*D:(j+1)*D]-m); l=l+p; ps.append(p.astype(BF))
-        p=jnp.concatenate(ps,axis=1)
+            p=jnp.exp2(sc[:,j*D:(j+1)*D]*SC-m); l=l+p; ps.append(p.astype(BF))
         mx[h]=m; ls[h]=l
+        return jnp.concatenate(ps,axis=1),al
+    def pv(h,s,g,p,al):
         acc[h]=acc[h]*al+jnp.dot(p,vb[s,g],preferred_element_type=F32)
     def wait_recv(s,g):
         for w in range(2): rcopy(w,s,g,partner,fsem.at[0,g,w],rsem.at[s,g,w]).wait_recv()
@@ -98,7 +99,14 @@
             @pl.when(direct)
             def _():
                 for w in range(2): fwd(s,g,w,dc).start()
-            for hh in range(grp): head_step(g*grp+hh,s,g)
+            sb[0]=qk(g*grp,s,g)
+            for hh in range(grp):
+                h=g*grp+hh
+                if hh+1<grp: sb[(hh+1)%2]=qk(h+1,s,g)
+                if hh>0: pv(h-1,s,g,pb[(hh-1)%2],albuf)
+                p,albuf=soft(h,sb[hh%2])
+                pb[hh%2]=p
+            pv(g*grp+grp-1,s,g,pb[(grp-1)%2],albuf)
         return 0
     lax.fori_loop(0,2*chip+core,shard_step,0)
     for h in range(nh):
@@ -123,16 +131,17 @@
         out_specs=vm,
         scratch_shapes=[pltpu.VMEM((nh,T,2*D),BF),pltpu.VMEM((n,nkv,2*D,T),BF),pltpu.VMEM((n,nkv,T,D),BF),
             pltpu.VMEM((nh,T,D),F32),pltpu.VMEM((nh,T,D),F32),pltpu.VMEM((nh,T,D),F32),
+            pltpu.VMEM((2,T,T),F32),pltpu.VMEM((2,T,T),BF),
             pltpu.SemaphoreType.DMA((n//2,nkv,2)),pltpu.SemaphoreType.DMA((n,nkv,2)),pltpu.SemaphoreType.DMA((n//2,nkv,2))],
         compiler_params=pltpu.CompilerParams(collective_id=1,has_side_effects=True,vmem_limit_bytes=56*1024*1024),
         cost_estimate=pl.CostEstimate(flops=4*T*T*n*HQ,bytes_accessed=4*T*HQ,transcendentals=T*T*n*nh),
         name="attn")(cu,q,kt,v)
 TW=256
 NB=5
-def front_body(n, pat_ref, emb_ref, slot_ref, cos_ref, sin_ref, lw_ref, lb_ref, w1_ref, b1_ref, w2_ref, b2_ref, na_ref, wq_ref, bq_ref, wk_ref, bk_ref, wv_ref, bv_ref,
+def front_body(n, pat_ref, emb_ref, slot_ref, rp_ref, lw_ref, lb_ref, w1_ref, b1_ref, w2_ref, b2_ref, na_ref, wq_ref, bq_ref, wk_ref, bk_ref, wv_ref, bv_ref,
                h0_ref, q_ref, kt_ref, v_ref,
                zf, z, inner, wbuf, mbuf, slots, onehot, hacc, wq, wk, wv,
-               wsem, qsem, slot_s, slot_r, own_s, fwd_s, rsem):
+               cs, sn, wsem, qsem, slot_s, slot_r, own_s, fwd_s, rsem):
     R=mbuf.shape[1]; T=emb_ref.shape[0]; V=pat_ref.shape[1]; K1=w1_ref.shape[0]; H=w2_ref.shape[1]
     n1=w1_ref.shape[1]//TW; n2=H//TW
     me=lax.axis_index('sp'); chip=me//2; core=lax.rem(me,2)
@@ -147,12 +156,14 @@
     def w1copy(t,s): return pltpu.make_async_copy(w1_ref.at[:,pl.ds(pl.multiple_of(t*TW,TW),TW)],wbuf.at[s],wsem.at[s])
     def w2copy(t,s): return pltpu.make_async_copy(w2_ref.at[:,pl.ds(pl.multiple_of(t*TW,TW),TW)],wbuf.at[s],wsem.at[s])
     for t in range(NB): w1copy(t,t).start()
+    slots[me]=jnp.broadcast_to(slot_ref[...].reshape(1,R),(8,R))
+    lw=lw_ref[...].astype(F32).reshape(1,V); lb=lb_ref[...].astype(F32).reshape(1,V)
     CH=128
     def ln(i,_):
         x=pat_ref[pl.ds(pl.multiple_of(i*CH,CH),CH),:].astype(F32)
         c=x-jnp.mean(x,axis=-1,keepdims=True)
         var=jnp.mean(c*c,axis=-1,keepdims=True)
-        y=c*lax.rsqrt(var+1e-6)*lw_ref[...].astype(F32)+lb_ref[...].astype(F32)
+        y=c*lax.rsqrt(var+1e-6)*lw+lb
         for p in range(V//D): zf[p]=y[:,p*D:(p+1)*D]
         for j in range(4):
             for p in range(V//D):
@@ -161,15 +172,14 @@
     lax.fori_loop(0,pat_ref.shape[0]//CH,ln,0)
     pl.semaphore_wait(bar,n-1)
     def slot_copy(d):
-        return pltpu.make_async_remote_copy(src_ref=slot_ref,dst_ref=slots.at[me],send_sem=slot_s.at[d-1],recv_sem=slot_r.at[me],device_id=dev(lax.rem(me+d,n)),device_id_type=MESH)
+        return pltpu.make_async_remote_copy(src_ref=slots.at[me],dst_ref=slots.at[me],send_sem=slot_s.at[d-1],recv_sem=slot_r.at[me],device_id=dev(lax.rem(me+d,n)),device_id_type=MESH)
     for d in range(1,n): slot_copy(d).start()
-    slots[me]=slot_ref[...]
     def first(i,_):
         s=lax.rem(i,NB)
         w1copy(i,s).wait()
         y=jnp.dot(z[...],wbuf[s],preferred_element_type=F32)
         cols=pl.ds(pl.multiple_of(i*TW,TW),TW)
-        y=y+b1_ref[:,cols].astype(F32)
+        y=y+b1_ref[cols].astype(F32).reshape(1,TW)
         inner[:,cols]=(0.5*y*(1.0+lax.erf(y*0.7071067811865476))).astype(BF)
         @pl.when(i+NB<n1)
         def _(): w1copy(i+NB,s).start()
@@ -184,14 +194,14 @@
     for j in range(n2):
         t=n1+j; s=t%NB
         w2copy(j,s).wait()
-        y=jnp.dot(inner[...],wbuf[s],preferred_element_type=F32)+b2_ref[:,j*TW:(j+1)*TW].astype(F32)
+        y=jnp.dot(inner[...],wbuf[s],preferred_element_type=F32)+b2_ref[j*TW:(j+1)*TW].astype(F32).reshape(1,TW)
         mbuf[me,:,j*TW:(j+1)*TW]=y.astype(BF)
         for a,tgt in enumerate((xn,yn,partner)): send(me,j,tgt,own_s.at[a,j]).start()
         if t+NB<n1+n2: w2copy(j+NB,s).start()
         elif t+NB==n1+n2: qc.start(); kc.start(); vc.start()
     for d in range(1,n):
         s=lax.rem(me+d,n)
-        pltpu.make_async_remote_copy(src_ref=slot_ref,dst_ref=slots.at[s],send_sem=slot_s.at[0],recv_sem=slot_r.at[s],device_id=dev(s),device_id_type=MESH).wait_recv()
+        pltpu.make_async_remote_copy(src_ref=slots.at[s],dst_ref=slots.at[s],send_sem=slot_s.at[0],recv_sem=slot_r.at[s],device_id=dev(s),device_id_type=MESH).wait_recv()
     base=me*T
     def oh(s,_):
         sl=slots[s][0:1,:]
@@ -205,6 +215,14 @@
         if firsttime: hacc[:,c]=p
         else: hacc[:,c]+=p
     for j in range(n2): place(me,j,True)
+    fi=lax.broadcasted_iota(jnp.int32,(D//2,T),0)
+    pos=jnp.where(fi<16,rp_ref[0:1,:],jnp.where(fi<40,rp_ref[1:2,:],rp_ref[2:3,:]))
+    fr=jnp.zeros((D//2,D),F32); fj=lax.broadcasted_iota(jnp.int32,(D//2,D),0)
+    for i in range(D//2): fr=jnp.where(fj==i,1000000.0**(-i/(D//2)),fr)
+    ang=pos.astype(F32)*fr[:,0:1]
+    cc=jnp.cos(ang); ss=jnp.sin(ang)
+    cs[...]=jnp.concatenate([cc,cc],axis=0).T
+    sn[...]=jnp.concatenate([-ss,ss],axis=0).T
     def arrive(s,j): send(s,j,partner,own_s.at[0,0]).wait_recv()
     fw=[]
     def forward(s,j,tgt,kind):
@@ -232,48 +250,38 @@
     has=jnp.sum(hit,axis=1,keepdims=True)>0.5
     h0=jnp.where(has,hacc[...],emb_ref[...].astype(F32))
     h0_ref[...]=h0.astype(BF)
-    a=(h0*lax.rsqrt(jnp.mean(h0*h0,axis=-1,keepdims=True)+1e-6)*na_ref[...].astype(F32)).astype(BF)
+    a=(h0*lax.rsqrt(jnp.mean(h0*h0,axis=-1,keepdims=True)+1e-6)*na_ref[...].astype(F32).reshape(1,H)).astype(BF)
     qc.wait(); kc.wait(); vc.wait()
     def rope(x):
-        return x*cos_ref[...]+pltpu.roll(x,D//2,1)*sin_ref[...]
+        return x*cs[...]+pltpu.roll(x,D//2,1)*sn[...]
     for i in range(H//TW):
-        y=jnp.dot(a,wq[:,i*TW:(i+1)*TW],preferred_element_type=F32)+bq_ref[:,i*TW:(i+1)*TW].astype(F32)
+        y=jnp.dot(a,wq[:,i*TW:(i+1)*TW],preferred_element_type=F32)+bq_ref[i*TW:(i+1)*TW].astype(F32).reshape(1,TW)
         for h in range(TW//D):
             q_ref[:,i*TW+h*D:i*TW+(h+1)*D]=rope(y[:,h*D:(h+1)*D]).astype(BF)
-    y=jnp.dot(a,wk[...],preferred_element_type=F32)+bk_ref[...].astype(F32)
+    y=jnp.dot(a,wk[...],preferred_element_type=F32)+bk_ref[...].astype(F32).reshape(1,-1)
     for h in range(wk.shape[1]//D):
         kt_ref[h*D:(h+1)*D,:]=rope(y[:,h*D:(h+1)*D]).T.astype(BF)
-    v_ref[...]=(jnp.dot(a,wv[...],preferred_element_type=F32)+bv_ref[...].astype(F32)).astype(BF)
+    v_ref[...]=(jnp.dot(a,wv[...],preferred_element_type=F32)+bv_ref[...].astype(F32).reshape(1,-1)).astype(BF)
     for d in range(1,n): slot_copy(d).wait_send()
     for j in range(n2):
         for a_,tgt in enumerate((xn,yn,partner)): send(me,j,tgt,own_s.at[a_,j]).wait_send()
     for c in fw: c.wait_send()
-def rope_tables(rope_pos):
-    inv_freq = 1000000.0 ** (-jnp.arange(0, 128, 2, dtype=jnp.float32) / 128)
-    fi = jnp.arange(64)[None, :]
-    chosen = jnp.where(fi < 16, rope_pos[0][:, None], jnp.where(fi < 40, rope_pos[1][:, None], rope_pos[2][:, None]))
-    ang = chosen.astype(jnp.float32) * inv_freq[None, :]
-    c, s = jnp.cos(ang), jnp.sin(ang)
-    return jnp.concatenate([c, c], axis=-1), jnp.concatenate([-s, s], axis=-1)
 def front_call(pat,emb,slot,rope_pos,lw,lb,w1,b1,w2,b2,na,wq,bq,wk,bk,wv,bv,n=8):
     T,H=emb.shape; R=slot.shape[0]; K1=w1.shape[0]; V=pat.shape[1]; KV=wk.shape[1]
-    cos,sin=rope_tables(rope_pos)
-    slot8=jnp.broadcast_to(slot[None,:],(8,R))
     vm=pl.BlockSpec(memory_space=pltpu.VMEM); hbm=pl.BlockSpec(memory_space=pl.ANY)
-    r1=lambda x: x.reshape(1,-1)
     n2=H//TW
     DS=pltpu.SemaphoreType.DMA
     return pl.pallas_call(functools.partial(front_body,n),
         out_shape=(jax.ShapeDtypeStruct((T,H),BF),jax.ShapeDtypeStruct((T,wq.shape[1]),BF),jax.ShapeDtypeStruct((KV,T),BF),jax.ShapeDtypeStruct((T,KV),BF)),
-        in_specs=[vm,vm,vm,vm,vm,vm,vm,hbm,vm,hbm,vm,vm,hbm,vm,hbm,vm,hbm,vm],
+        in_specs=[vm,vm,vm,vm,vm,vm,hbm,vm,hbm,vm,vm,hbm,vm,hbm,vm,hbm,vm],
         out_specs=(vm,)*4,
         scratch_shapes=[pltpu.VMEM((V//D,128,D),F32),pltpu.VMEM((R,K1),BF),pltpu.VMEM((R,w1.shape[1]),BF),pltpu.VMEM((NB,K1,TW),BF),
             pltpu.VMEM((n,R,H),BF),pltpu.VMEM((n,8,R),jnp.int32),pltpu.VMEM((n,T,R),BF),pltpu.VMEM((T,H),F32),
-            pltpu.VMEM(wq.shape,BF),pltpu.VMEM(wk.shape,BF),pltpu.VMEM(wv.shape,BF),
+            pltpu.VMEM(wq.shape,BF),pltpu.VMEM(wk.shape,BF),pltpu.VMEM(wv.shape,BF),pltpu.VMEM((T,D),F32),pltpu.VMEM((T,D),F32),
             DS((NB,)),DS((3,)),DS((n-1,)),DS((n,)),DS((3,n2)),DS((4,n2)),DS((n,n2))],
         compiler_params=pltpu.CompilerParams(collective_id=2,has_side_effects=True,vmem_limit_bytes=62*1024*1024),
         cost_estimate=pl.CostEstimate(flops=2*R*K1*(K1+H),bytes_accessed=2*K1*(K1+H),transcendentals=R*K1),
-        name="front")(pat,emb,slot8,cos,sin,r1(lw),r1(lb),w1,r1(b1),w2,r1(b2),r1(na),wq,r1(bq),wk,r1(bk),wv,r1(bv))
+        name="front")(pat,emb,slot,rope_pos,lw,lb,w1,b1,w2,b2,na,wq,bq,wk,bk,wv,bv)
 def mlp_body(nsub, h0_ref, at_ref, wo_ref, nm_ref, wg_ref, wu_ref, wd_ref, out_ref, b_scr, acc_scr):
     i=pl.program_id(0)
     @pl.when(i==0)
@@ -283,7 +291,7 @@
             h1=(h0_ref[rows,:].astype(F32)+jnp.dot(at_ref[rows,:],wo_ref[...],preferred_element_type=F32)).astype(BF)
             h1w=h1.astype(F32)
             acc_scr[rows,:]=h1w
-            b_scr[rows,:]=(h1w*lax.rsqrt(jnp.mean(h1w*h1w,axis=-1,keepdims=True)+1e-6)*nm_ref[...].astype(F32)).astype(BF)
+            b_scr[rows,:]=(h1w*lax.rsqrt(jnp.mean(h1w*h1w,axis=-1,keepdims=True)+1e-6)*nm_ref[...].astype(F32).reshape(1,-1)).astype(BF)
     b=b_scr[...]
     tf=wg_ref.shape[1]; sub=tf//nsub
     acts=[]
@@ -303,14 +311,14 @@
     return pl.pallas_call(functools.partial(mlp_body,nsub),
         out_shape=jax.ShapeDtypeStruct((T,H),BF),
         grid=(Fd//tf,),
-        in_specs=[full((T,H)),full((T,H)),full((H,H)),full((1,H)),
+        in_specs=[full((T,H)),full((T,H)),full((H,H)),pl.BlockSpec(memory_space=pltpu.VMEM),
                   pl.BlockSpec((H,tf),lambda i:(0,i)),pl.BlockSpec((H,tf),lambda i:(0,i)),pl.BlockSpec((tf,H),lambda i:(i,0))],
         out_specs=pl.BlockSpec((T,H),lambda i:(0,0),pipeline_mode=pl.Buffered(1)),
         scratch_shapes=[pltpu.VMEM((T,H),BF),pltpu.VMEM((T,H),F32)],
         compiler_params=pltpu.CompilerParams(dimension_semantics=("arbitrary",),vmem_limit_bytes=60*1024*1024),
         cost_estimate=pl.CostEstimate(flops=2*T*H*(H+3*Fd),bytes_accessed=2*H*(H+3*Fd),transcendentals=T*Fd),
         name="mlp",
-    )(h0,at,wo,nm.reshape(1,H),wg,wu,wd)
+    )(h0,at,wo,nm,wg,wu,wd)
 
 
 def solution(mesh):

time: 187 us -> 163 us (0.87)
  local copies, waits for them, and re-layouts: 12.9 us -> 0 us
  Pallas kernels: 171 us -> 163 us
  other arithmetic: 2.75 us -> 0 us
    reshape x9 -> x0, local copies, waits for them, and re-layouts: 10.8 us -> none  [the longest x8 10.2 us: front_call(): r1 = lambda x: x.reshape(1, -1)]
    pallas_call x1, Pallas kernels: 54.8 us -> 47.1 us  [attn_call(): pl.pallas_call(functools.partial(attn_body, n, nh, nkv), out_shape=jax.Sh...]
where the time goes in v2:
time: 163 us
  Pallas kernels  163 us (100%)
    pallas_call x1, Pallas kernels, front_call(): pl.pallas_call(functools.partial(front_body, n), out_shape=(jax.ShapeDtyp...  59.9 us
    pallas_call x1, Pallas kernels, mlp_call(): pl.pallas_call(functools.partial(mlp_body, nsub), out_shape=jax.ShapeDtyp...  56.1 us
    pallas_call x1, Pallas kernels, attn_call(): pl.pallas_call(functools.partial(attn_body, n, nh, nkv), out_shape=jax.Sh...  47.1 us

profile of v2, /device:TPU:7, one launch (start us, length us, event | category | flops | bytes accessed | tf_op | source)
XLA Modules:
  0.0 163.2 jit_solution(2725317613999220678)
XLA Ops:
  0.0 59.9 %front.1 = (bf16[512,1536]{1,0:T(8,128)(2,1)}, bf16[512,1536]{1,0:T(8,128)(2,1)}, bf16[256,512]{1,0:T(8,128)(2,1)}, bf16[512,256]{1,0:T(8,128)(2,1)}) custom-call(bf16[1024,1280]{1,0:T(8,128)(2,1)} %pat_ref.1, bf16[512,1536]{1,0:T(8,128)(2,1)} %emb_ref.1, s32[256]{0:T(256)} %slot_ref.1, s32[3,512]{1,0:T(4,128)} %rp_ref.1, bf16[1280]{0:T(1024)(128)(2,1)} %lw_ref.1, ...), custom_call_target="tpu_custom_call" | custom-call | flops 17448304640 | bytes 68157440 | tf_op jit(solution)/shard_map/front/pallas_call | solution.py:274
  60.0 47.1 %attn.1.at_ref = bf16[512,1536]{1,0:T(8,128)(2,1)} custom-call(s32[3]{0:T(128)} %cu_ref.1, bf16[512,1536]{1,0:T(8,128)(2,1)} %get-tuple-element.10.q_ref, bf16[256,512]{1,0:T(8,128)(2,1)} %get-tuple-element.11.kt_ref, bf16[512,256]{1,0:T(8,128)(2,1)} %get-tuple-element.12.v_ref), custom_call_target="tpu_custom_call" | custom-call | flops 12884901888 | bytes 3145728 | tf_op jit(solution)/shard_map/attn/pallas_call | solution.py:128
  107.1 56.1 %mlp.1 = bf16[512,1536]{1,0:T(8,128)(2,1)} custom-call(bf16[512,1536]{1,0:T(8,128)(2,1)} %get-tuple-element.9.h0_ref, bf16[512,1536]{1,0:T(8,128)(2,1)} %attn.1.at_ref, bf16[1536,1536]{1,0:T(8,128)(2,1)} %wo_ref.1, bf16[1536]{0:T(1024)(128)(2,1)} %nm_ref.1, bf16[1536,8960]{1,0:T(8,128)(2,1)} %wg_ref.1, bf16[1536,8960]{1,0:T(8,128)(2,1)} %wu_ref.1, ...), custom_call_target="tpu_custom_call" | custom-call | flops 44694503424 | bytes 87293952 | tf_op jit(solution)/shard_map/mlp/pallas_call | solution.py:311

commit v3 on v2

--- a/solution.py
+++ b/solution.py
@@ -51,29 +51,13 @@
         kt=kt.astype(BF)
         for g in range(nkv): kb[s,g,pl.ds(D,D),:]=kt
         return 0
-    lax.fori_loop(0,n,fill,0)
+    lax.fori_loop(0,me+1,fill,0)
     for h in range(nh):
         qa[h,:,:D]=q_ref[:,h*D:(h+1)*D]
         qa[h,:,D:]=tail
     for g in range(nkv):
         kb[me,g,pl.ds(0,D),:]=kt_ref[g*D:(g+1)*D,:]
-    HB=T//2
-    def own(h,_):
-        g=h//grp
-        for r in range(2):
-            rows=pl.ds(r*HB,HB); W=(r+1)*HB
-            s=jnp.dot(qa[h,rows,:],kb[me,g,:,pl.ds(0,W)],preferred_element_type=F32)*SC
-            qi=lax.broadcasted_iota(jnp.int32,(HB,W),0)+r*HB; ki=lax.broadcasted_iota(jnp.int32,(HB,W),1)
-            s=jnp.where(ki<=qi,s,-1e30)
-            m=jnp.max(s,axis=1,keepdims=True)
-            p=jnp.exp2(s-m)
-            l=p[:,:D]
-            for j in range(1,W//D): l=l+p[:,j*D:(j+1)*D]
-            mx[h,rows,:]=jnp.broadcast_to(m,(HB,D)); ls[h,rows,:]=l
-            vg=v_ref[pl.ds(0,W),pl.ds(pl.multiple_of(g*D,D),D)]
-            acc[h,rows,:]=jnp.dot(p.astype(BF),vg,preferred_element_type=F32)
-        return 0
-    lax.fori_loop(0,nh,own,0)
+        vb[me,g]=v_ref[:,g*D:(g+1)*D]
     def qk(h,s,g): return jnp.dot(qa[h],kb[s,g],preferred_element_type=F32)
     def soft(h,sc):
         mp=mx[h]
@@ -86,6 +70,28 @@
         return jnp.concatenate(ps,axis=1),al
     def pv(h,s,g,p,al):
         acc[h]=acc[h]*al+jnp.dot(p,vb[s,g],preferred_element_type=F32)
+    def soft_own(h,sc):
+        qi=lax.broadcasted_iota(jnp.int32,(T,T),0); ki=lax.broadcasted_iota(jnp.int32,(T,T),1)
+        sc=jnp.where(ki<=qi,sc,-1e30)
+        m=jnp.broadcast_to(jnp.max(sc,axis=1,keepdims=True)*SC,(T,D))
+        l=None; ps=[]
+        for j in range(T//D):
+            p=jnp.exp2(sc[:,j*D:(j+1)*D]*SC-m); l=p if l is None else l+p
+            ps.append(p.astype(BF))
+        mx[h]=m; ls[h]=l
+        return jnp.concatenate(ps,axis=1)
+    def pv_own(h,g,p): acc[h]=jnp.dot(p,vb[me,g],preferred_element_type=F32)
+    def own(g,_):
+        h0=g*grp
+        sb[0]=qk(h0,me,g)
+        for hh in range(grp):
+            h=h0+hh
+            if hh+1<grp: sb[(hh+1)%2]=qk(h+1,me,g)
+            if hh>0: pv_own(h-1,g,pb[(hh-1)%2])
+            pb[hh%2]=soft_own(h,sb[hh%2])
+        pv_own(h0+grp-1,g,pb[(grp-1)%2])
+        return 0
+    lax.fori_loop(0,nkv,own,0)
     def wait_recv(s,g):
         for w in range(2): rcopy(w,s,g,partner,fsem.at[0,g,w],rsem.at[s,g,w]).wait_recv()
     def fwd(s,g,w,dc): return rcopy(w,s,g,partner,fsem.at[dc,g,w],rsem.at[s,g,w])
@@ -94,7 +100,7 @@
         dc=jnp.where(j<0,0,j//2+1)
         direct=(j>=0)&(lax.rem(j+2,2)==0)
         s=jnp.where(j<0,partner,(chip-dc)*2+jnp.where(direct,core,1-core))
-        for g in range(nkv):
+        def per_g(g,_):
             wait_recv(s,g)
             @pl.when(direct)
             def _():
@@ -107,6 +113,8 @@
                 p,albuf=soft(h,sb[hh%2])
                 pb[hh%2]=p
             pv(g*grp+grp-1,s,g,pb[(grp-1)%2],albuf)
+            return 0
+        lax.fori_loop(0,nkv,per_g,0)
         return 0
     lax.fori_loop(0,2*chip+core,shard_step,0)
     for h in range(nh):
@@ -188,17 +196,21 @@
         return 0
     lax.fori_loop(0,n1,first,0)
     qc=pltpu.make_async_copy(wq_ref,wq,qsem.at[0]); kc=pltpu.make_async_copy(wk_ref,wk,qsem.at[1]); vc=pltpu.make_async_copy(wv_ref,wv,qsem.at[2])
-    def tile(s,j): return mbuf.at[s,:,pl.ds(j*TW,TW)]
+    def tile(s,j): return mbuf.at[s,:,pl.ds(pl.multiple_of(j*TW,TW) if not isinstance(j,int) else j*TW,TW)]
     def send(src,j,tgt,ss):
         return pltpu.make_async_remote_copy(src_ref=tile(src,j),dst_ref=tile(src,j),send_sem=ss,recv_sem=rsem.at[src,j],device_id=dev(tgt),device_id_type=MESH)
-    for j in range(n2):
-        t=n1+j; s=t%NB
+    def jcols(j): return pl.ds(pl.multiple_of(j*TW,TW),TW) if not isinstance(j,int) else pl.ds(j*TW,TW)
+    def second(j,_):
+        s=lax.rem(n1+j,NB)
         w2copy(j,s).wait()
-        y=jnp.dot(inner[...],wbuf[s],preferred_element_type=F32)+b2_ref[j*TW:(j+1)*TW].astype(F32).reshape(1,TW)
-        mbuf[me,:,j*TW:(j+1)*TW]=y.astype(BF)
+        y=jnp.dot(inner[...],wbuf[s],preferred_element_type=F32)+b2_ref[jcols(j)].astype(F32).reshape(1,TW)
+        mbuf[me,:,jcols(j)]=y.astype(BF)
         for a,tgt in enumerate((xn,yn,partner)): send(me,j,tgt,own_s.at[a,j]).start()
-        if t+NB<n1+n2: w2copy(j+NB,s).start()
-        elif t+NB==n1+n2: qc.start(); kc.start(); vc.start()
+        @pl.when(j+NB<n2)
+        def _(): w2copy(j+NB,s).start()
+        return 0
+    qc.start(); kc.start(); vc.start()
+    lax.fori_loop(0,n2,second,0)
     for d in range(1,n):
         s=lax.rem(me+d,n)
         pltpu.make_async_remote_copy(src_ref=slots.at[s],dst_ref=slots.at[s],send_sem=slot_s.at[0],recv_sem=slot_r.at[s],device_id=dev(s),device_id_type=MESH).wait_recv()
@@ -282,43 +294,47 @@
         compiler_params=pltpu.CompilerParams(collective_id=2,has_side_effects=True,vmem_limit_bytes=62*1024*1024),
         cost_estimate=pl.CostEstimate(flops=2*R*K1*(K1+H),bytes_accessed=2*K1*(K1+H),transcendentals=R*K1),
         name="front")(pat,emb,slot,rope_pos,lw,lb,w1,b1,w2,b2,na,wq,bq,wk,bk,wv,bv)
-def mlp_body(nsub, h0_ref, at_ref, wo_ref, nm_ref, wg_ref, wu_ref, wd_ref, out_ref, b_scr, acc_scr):
-    i=pl.program_id(0)
-    @pl.when(i==0)
-    def _():
-        for r in range(2):
-            rows=pl.ds(r*256,256)
-            h1=(h0_ref[rows,:].astype(F32)+jnp.dot(at_ref[rows,:],wo_ref[...],preferred_element_type=F32)).astype(BF)
-            h1w=h1.astype(F32)
-            acc_scr[rows,:]=h1w
-            b_scr[rows,:]=(h1w*lax.rsqrt(jnp.mean(h1w*h1w,axis=-1,keepdims=True)+1e-6)*nm_ref[...].astype(F32).reshape(1,-1)).astype(BF)
-    b=b_scr[...]
-    tf=wg_ref.shape[1]; sub=tf//nsub
-    acts=[]
-    for j in range(nsub):
-        cols=slice(j*sub,(j+1)*sub)
-        g=jnp.dot(b,wg_ref[:,cols],preferred_element_type=F32)
-        u=jnp.dot(b,wu_ref[:,cols],preferred_element_type=F32)
-        acts.append((g*jax.nn.sigmoid(g)*u).astype(BF))
-    a=jnp.concatenate(acts,axis=1) if nsub>1 else acts[0]
-    acc_scr[...]+=jnp.dot(a,wd_ref[...],preferred_element_type=F32)
-    @pl.when(i==pl.num_programs(0)-1)
-    def _():
-        out_ref[...]=acc_scr[...].astype(BF)
-def mlp_call(h0,at,wo,nm,wg,wu,wd,tf=1280,nsub=5):
+def mlp_body(h0_ref, at_ref, wo_ref, nm_ref, wg_ref, wu_ref, wd_ref, out_ref, h0, at, wo, wg, wu, wd, b, acc, sem):
+    T,H=h0.shape; TF=wg.shape[2]; ns=wg_ref.shape[1]//TF
+    first=[pltpu.make_async_copy(s,d,sem.at[2,i]) for i,(s,d) in enumerate(((at_ref,at),(wo_ref,wo),(h0_ref,h0)))]
+    for c in first: c.start()
+    cols=lambda i: pl.ds(pl.multiple_of(i*TF,TF),TF)
+    def copies(i,k): return (pltpu.make_async_copy(wg_ref.at[:,cols(i)],wg.at[k],sem.at[k,0]),pltpu.make_async_copy(wu_ref.at[:,cols(i)],wu.at[k],sem.at[k,1]),pltpu.make_async_copy(wd_ref.at[cols(i),:],wd.at[k],sem.at[k,2]))
+    for k in range(2):
+        for c in copies(k,k): c.start()
+    for c in first: c.wait()
+    HT=T//2
+    for r in range(2):
+        rows=pl.ds(r*HT,HT)
+        h1=(h0[rows,:].astype(F32)+jnp.dot(at[rows,:],wo[...],preferred_element_type=F32)).astype(BF).astype(F32)
+        acc[rows,:]=h1
+        b[rows,:]=(h1*lax.rsqrt(jnp.mean(h1*h1,axis=-1,keepdims=True)+1e-6)*nm_ref[...].astype(F32).reshape(1,H)).astype(BF)
+    def step(i,_):
+        k=lax.rem(i,2)
+        for c in copies(i,k): c.wait()
+        x=b[...]
+        g=jnp.dot(x,wg[k],preferred_element_type=F32)
+        u=jnp.dot(x,wu[k],preferred_element_type=F32)
+        a=(g*jax.nn.sigmoid(g)*u).astype(BF)
+        acc[...]+=jnp.dot(a,wd[k],preferred_element_type=F32)
+        @pl.when(i+2<ns)
+        def _():
+            for c in copies(i+2,k): c.start()
+        return 0
+    lax.fori_loop(0,ns,step,0)
+    out_ref[...]=acc[...].astype(BF)
+def mlp_call(h0,at,wo,nm,wg,wu,wd,tf=1280):
     T,H=h0.shape; Fd=wg.shape[1]
-    full=lambda s: pl.BlockSpec(s,lambda i:(0,)*len(s),pipeline_mode=pl.Buffered(1))
-    return pl.pallas_call(functools.partial(mlp_body,nsub),
+    hbm=pl.BlockSpec(memory_space=pl.ANY); vm=pl.BlockSpec(memory_space=pltpu.VMEM)
+    V=pltpu.VMEM
+    return pl.pallas_call(mlp_body,
         out_shape=jax.ShapeDtypeStruct((T,H),BF),
-        grid=(Fd//tf,),
-        in_specs=[full((T,H)),full((T,H)),full((H,H)),pl.BlockSpec(memory_space=pltpu.VMEM),
-                  pl.BlockSpec((H,tf),lambda i:(0,i)),pl.BlockSpec((H,tf),lambda i:(0,i)),pl.BlockSpec((tf,H),lambda i:(i,0))],
-        out_specs=pl.BlockSpec((T,H),lambda i:(0,0),pipeline_mode=pl.Buffered(1)),
-        scratch_shapes=[pltpu.VMEM((T,H),BF),pltpu.VMEM((T,H),F32)],
-        compiler_params=pltpu.CompilerParams(dimension_semantics=("arbitrary",),vmem_limit_bytes=60*1024*1024),
+        in_specs=[hbm,hbm,hbm,vm,hbm,hbm,hbm],
+        out_specs=vm,
+        scratch_shapes=[V((T,H),BF),V(at.shape,BF),V(wo.shape,BF),V((2,H,tf),BF),V((2,H,tf),BF),V((2,tf,H),BF),V((T,H),BF),V((T,H),F32),pltpu.SemaphoreType.DMA((3,3))],
+        compiler_params=pltpu.CompilerParams(vmem_limit_bytes=60*1024*1024),
         cost_estimate=pl.CostEstimate(flops=2*T*H*(H+3*Fd),bytes_accessed=2*H*(H+3*Fd),transcendentals=T*Fd),
-        name="mlp",
-    )(h0,at,wo,nm,wg,wu,wd)
+        name="mlp")(h0,at,wo,nm,wg,wu,wd)
 
 
 def solution(mesh):

time: 163 us -> 156 us (0.957)
  Pallas kernels: 163 us -> 156 us
    pallas_call x1, Pallas kernels: 56.1 us -> 52.6 us  [mlp_call(): pl.pallas_call(mlp_body, out_shape=jax.ShapeDtypeStruct((T, H), BF), in_s...]
    pallas_call x1, Pallas kernels: 47.1 us -> 43.7 us  [attn_call(): pl.pallas_call(functools.partial(attn_body, n, nh, nkv), out_shape=jax.Sh...]
where the time goes in v3:
time: 156 us
  Pallas kernels  156 us (100%)
    pallas_call x1, Pallas kernels, front_call(): pl.pallas_call(functools.partial(front_body, n), out_shape=(jax.ShapeDtyp...  59.3 us
    pallas_call x1, Pallas kernels, mlp_call(): pl.pallas_call(mlp_body, out_shape=jax.ShapeDtypeStruct((T, H), BF), in_s...  52.6 us
    pallas_call x1, Pallas kernels, attn_call(): pl.pallas_call(functools.partial(attn_body, n, nh, nkv), out_shape=jax.Sh...  43.7 us

profile of v3, /device:TPU:7, one launch (start us, length us, event | category | flops | bytes accessed | tf_op | source)
XLA Modules:
  0.0 155.7 jit_solution(6777357010364155373)
XLA Ops:
  0.0 59.3 %front.1 = (bf16[512,1536]{1,0:T(8,128)(2,1)}, bf16[512,1536]{1,0:T(8,128)(2,1)}, bf16[256,512]{1,0:T(8,128)(2,1)}, bf16[512,256]{1,0:T(8,128)(2,1)}) custom-call(bf16[1024,1280]{1,0:T(8,128)(2,1)} %pat_ref.1, bf16[512,1536]{1,0:T(8,128)(2,1)} %emb_ref.1, s32[256]{0:T(256)} %slot_ref.1, s32[3,512]{1,0:T(4,128)} %rp_ref.1, bf16[1280]{0:T(1024)(128)(2,1)} %lw_ref.1, ...), custom_call_target="tpu_custom_call" | custom-call | flops 17448304640 | bytes 68157440 | tf_op jit(solution)/shard_map/front/pallas_call | solution.py:286
  59.3 43.7 %attn.1.at_ref = bf16[512,1536]{1,0:T(8,128)(2,1)} custom-call(s32[3]{0:T(128)} %cu_ref.1, bf16[512,1536]{1,0:T(8,128)(2,1)} %get-tuple-element.10.q_ref, bf16[256,512]{1,0:T(8,128)(2,1)} %get-tuple-element.11.kt_ref, bf16[512,256]{1,0:T(8,128)(2,1)} %get-tuple-element.12.v_ref), custom_call_target="tpu_custom_call" | custom-call | flops 12884901888 | bytes 3145728 | tf_op jit(solution)/shard_map/attn/pallas_call | solution.py:136
  103.0 52.6 %mlp.1 = bf16[512,1536]{1,0:T(8,128)(2,1)} custom-call(bf16[512,1536]{1,0:T(8,128)(2,1)} %get-tuple-element.9.h0_ref, bf16[512,1536]{1,0:T(8,128)(2,1)} %attn.1.at_ref, bf16[1536,1536]{1,0:T(8,128)(2,1)} %wo_ref.1, bf16[1536]{0:T(1024)(128)(2,1)} %nm_ref.1, bf16[1536,8960]{1,0:T(8,128)(2,1)} %wg_ref.1, bf16[1536,8960]{1,0:T(8,128)(2,1)} %wu_ref.1, ...), custom_call_target="tpu_custom_call" | custom-call | flops 44694503424 | bytes 87293952 | tf_op jit(solution)/shard_map/mlp/pallas_call | solution.py:330

commit v4 on v3

--- a/solution.py
+++ b/solution.py
@@ -105,14 +105,14 @@
             @pl.when(direct)
             def _():
                 for w in range(2): fwd(s,g,w,dc).start()
-            sb[0]=qk(g*grp,s,g)
+            sb[0]=qk(g*grp,s,g); pal=None
             for hh in range(grp):
                 h=g*grp+hh
+                if hh>0: pv(h-1,s,g,pb[(hh-1)%2],pal)
                 if hh+1<grp: sb[(hh+1)%2]=qk(h+1,s,g)
-                if hh>0: pv(h-1,s,g,pb[(hh-1)%2],albuf)
-                p,albuf=soft(h,sb[hh%2])
+                p,pal=soft(h,sb[hh%2])
                 pb[hh%2]=p
-            pv(g*grp+grp-1,s,g,pb[(grp-1)%2],albuf)
+            pv(g*grp+grp-1,s,g,pb[(grp-1)%2],pal)
             return 0
         lax.fori_loop(0,nkv,per_g,0)
         return 0
@@ -149,7 +149,7 @@
 def front_body(n, pat_ref, emb_ref, slot_ref, rp_ref, lw_ref, lb_ref, w1_ref, b1_ref, w2_ref, b2_ref, na_ref, wq_ref, bq_ref, wk_ref, bk_ref, wv_ref, bv_ref,
                h0_ref, q_ref, kt_ref, v_ref,
                zf, z, inner, wbuf, mbuf, slots, onehot, hacc, wq, wk, wv,
-               cs, sn, wsem, qsem, slot_s, slot_r, own_s, fwd_s, rsem):
+               cs, sn, h0b, qb, osem, wsem, qsem, slot_s, slot_r, own_s, fwd_s, rsem):
     R=mbuf.shape[1]; T=emb_ref.shape[0]; V=pat_ref.shape[1]; K1=w1_ref.shape[0]; H=w2_ref.shape[1]
     n1=w1_ref.shape[1]//TW; n2=H//TW
     me=lax.axis_index('sp'); chip=me//2; core=lax.rem(me,2)
@@ -221,12 +221,15 @@
         onehot[s]=jnp.where(tok==sl,1.0,0.0).astype(BF)
         return 0
     lax.fori_loop(0,n,oh,0)
-    def place(s,j,firsttime=False):
+    def place(s,j):
         c=slice(j*TW,(j+1)*TW)
         p=jnp.dot(onehot[s],mbuf[s,:,c],preferred_element_type=F32)
-        if firsttime: hacc[:,c]=p
-        else: hacc[:,c]+=p
-    for j in range(n2): place(me,j,True)
+        hacc[:,c]+=p
+    hit=onehot[0].astype(F32)
+    for s in range(1,n): hit=hit+onehot[s].astype(F32)
+    has=jnp.sum(hit,axis=1,keepdims=True)>0.5
+    hacc[...]=jnp.where(has,0.0,emb_ref[...].astype(F32))
+    for j in range(n2): place(me,j)
     fi=lax.broadcasted_iota(jnp.int32,(D//2,T),0)
     pos=jnp.where(fi<16,rp_ref[0:1,:],jnp.where(fi<40,rp_ref[1:2,:],rp_ref[2:3,:]))
     fr=jnp.zeros((D//2,D),F32); fj=lax.broadcasted_iota(jnp.int32,(D//2,D),0)
@@ -257,11 +260,9 @@
         arrive(dg,j); forward(dg,j,partner,3); place(dg,j)
         if j>0: arrive(other(dg),j-1); place(other(dg),j-1)
     arrive(other(dg),n2-1); place(other(dg),n2-1)
-    hit=onehot[0].astype(F32)
-    for s in range(1,n): hit=hit+onehot[s].astype(F32)
-    has=jnp.sum(hit,axis=1,keepdims=True)>0.5
-    h0=jnp.where(has,hacc[...],emb_ref[...].astype(F32))
-    h0_ref[...]=h0.astype(BF)
+    h0=hacc[...]
+    h0b[...]=h0.astype(BF)
+    outs=[pltpu.make_async_copy(h0b,h0_ref,osem.at[0])]; outs[0].start()
     a=(h0*lax.rsqrt(jnp.mean(h0*h0,axis=-1,keepdims=True)+1e-6)*na_ref[...].astype(F32).reshape(1,H)).astype(BF)
     qc.wait(); kc.wait(); vc.wait()
     def rope(x):
@@ -269,11 +270,13 @@
     for i in range(H//TW):
         y=jnp.dot(a,wq[:,i*TW:(i+1)*TW],preferred_element_type=F32)+bq_ref[i*TW:(i+1)*TW].astype(F32).reshape(1,TW)
         for h in range(TW//D):
-            q_ref[:,i*TW+h*D:i*TW+(h+1)*D]=rope(y[:,h*D:(h+1)*D]).astype(BF)
+            qb[:,i*TW+h*D:i*TW+(h+1)*D]=rope(y[:,h*D:(h+1)*D]).astype(BF)
+        o=pltpu.make_async_copy(qb.at[:,pl.ds(i*TW,TW)],q_ref.at[:,pl.ds(i*TW,TW)],osem.at[1+i]); o.start(); outs.append(o)
     y=jnp.dot(a,wk[...],preferred_element_type=F32)+bk_ref[...].astype(F32).reshape(1,-1)
     for h in range(wk.shape[1]//D):
         kt_ref[h*D:(h+1)*D,:]=rope(y[:,h*D:(h+1)*D]).T.astype(BF)
     v_ref[...]=(jnp.dot(a,wv[...],preferred_element_type=F32)+bv_ref[...].astype(F32).reshape(1,-1)).astype(BF)
+    for o in outs: o.wait()
     for d in range(1,n): slot_copy(d).wait_send()
     for j in range(n2):
         for a_,tgt in enumerate((xn,yn,partner)): send(me,j,tgt,own_s.at[a_,j]).wait_send()
@@ -286,10 +289,10 @@
     return pl.pallas_call(functools.partial(front_body,n),
         out_shape=(jax.ShapeDtypeStruct((T,H),BF),jax.ShapeDtypeStruct((T,wq.shape[1]),BF),jax.ShapeDtypeStruct((KV,T),BF),jax.ShapeDtypeStruct((T,KV),BF)),
         in_specs=[vm,vm,vm,vm,vm,vm,hbm,vm,hbm,vm,vm,hbm,vm,hbm,vm,hbm,vm],
-        out_specs=(vm,)*4,
+        out_specs=(hbm,hbm,vm,vm),
         scratch_shapes=[pltpu.VMEM((V//D,128,D),F32),pltpu.VMEM((R,K1),BF),pltpu.VMEM((R,w1.shape[1]),BF),pltpu.VMEM((NB,K1,TW),BF),
             pltpu.VMEM((n,R,H),BF),pltpu.VMEM((n,8,R),jnp.int32),pltpu.VMEM((n,T,R),BF),pltpu.VMEM((T,H),F32),
-            pltpu.VMEM(wq.shape,BF),pltpu.VMEM(wk.shape,BF),pltpu.VMEM(wv.shape,BF),pltpu.VMEM((T,D),F32),pltpu.VMEM((T,D),F32),
+            pltpu.VMEM(wq.shape,BF),pltpu.VMEM(wk.shape,BF),pltpu.VMEM(wv.shape,BF),pltpu.VMEM((T,D),F32),pltpu.VMEM((T,D),F32),pltpu.VMEM((T,H),BF),pltpu.VMEM((T,wq.shape[1]),BF),DS((1+n2,)),
             DS((NB,)),DS((3,)),DS((n-1,)),DS((n,)),DS((3,n2)),DS((4,n2)),DS((n,n2))],
         compiler_params=pltpu.CompilerParams(collective_id=2,has_side_effects=True,vmem_limit_bytes=62*1024*1024),
         cost_estimate=pl.CostEstimate(flops=2*R*K1*(K1+H),bytes_accessed=2*K1*(K1+H),transcendentals=R*K1),

time: 156 us -> 155 us (level)
  no operation moved by 1% of the time
where the time goes in v4:
time: 155 us
  Pallas kernels  155 us (100%)
    pallas_call x1, Pallas kernels, front_call(): pl.pallas_call(functools.partial(front_body, n), out_shape=(jax.ShapeDtyp...  58.9 us
    pallas_call x1, Pallas kernels, mlp_call(): pl.pallas_call(mlp_body, out_shape=jax.ShapeDtypeStruct((T, H), BF), in_s...  52.6 us
    pallas_call x1, Pallas kernels, attn_call(): pl.pallas_call(functools.partial(attn_body, n, nh, nkv), out_shape=jax.Sh...  43.3 us

profile of v4, /device:TPU:7, one launch (start us, length us, event | category | flops | bytes accessed | tf_op | source)
XLA Modules:
  0.0 154.9 jit_solution(16391369312980800590)
XLA Ops:
  0.0 58.9 %front.1 = (bf16[512,1536]{1,0:T(8,128)(2,1)}, bf16[512,1536]{1,0:T(8,128)(2,1)}, bf16[256,512]{1,0:T(8,128)(2,1)}, bf16[512,256]{1,0:T(8,128)(2,1)}) custom-call(bf16[1024,1280]{1,0:T(8,128)(2,1)} %pat_ref.1, bf16[512,1536]{1,0:T(8,128)(2,1)} %emb_ref.1, s32[256]{0:T(256)} %slot_ref.1, s32[3,512]{1,0:T(4,128)} %rp_ref.1, bf16[1280]{0:T(1024)(128)(2,1)} %lw_ref.1, ...), custom_call_target="tpu_custom_call" | custom-call | flops 17448304640 | bytes 68157440 | tf_op jit(solution)/shard_map/front/pallas_call | solution.py:289
  58.9 43.3 %attn.1.at_ref = bf16[512,1536]{1,0:T(8,128)(2,1)} custom-call(s32[3]{0:T(128)} %cu_ref.1, bf16[512,1536]{1,0:T(8,128)(2,1)} %get-tuple-element.10.q_ref, bf16[256,512]{1,0:T(8,128)(2,1)} %get-tuple-element.11.kt_ref, bf16[512,256]{1,0:T(8,128)(2,1)} %get-tuple-element.12.v_ref), custom_call_target="tpu_custom_call" | custom-call | flops 12884901888 | bytes 3145728 | tf_op jit(solution)/shard_map/attn/pallas_call | solution.py:136
  102.2 52.6 %mlp.1 = bf16[512,1536]{1,0:T(8,128)(2,1)} custom-call(bf16[512,1536]{1,0:T(8,128)(2,1)} %get-tuple-element.9.h0_ref, bf16[512,1536]{1,0:T(8,128)(2,1)} %attn.1.at_ref, bf16[1536,1536]{1,0:T(8,128)(2,1)} %wo_ref.1, bf16[1536]{0:T(1024)(128)(2,1)} %nm_ref.1, bf16[1536,8960]{1,0:T(8,128)(2,1)} %wg_ref.1, bf16[1536,8960]{1,0:T(8,128)(2,1)} %wu_ref.1, ...), custom_call_target="tpu_custom_call" | custom-call | flops 44694503424 | bytes 87293952 | tf_op jit(solution)/shard_map/mlp/pallas_call | solution.py:333
